TPU v7x, 512 devices: a 4x2x32 block of a 4x16x32 slice. The times are simulated.
512 devices in a mesh: group: 2 (over y), tm: 32 (over z), space: 4 (over x), head: 2 (over core).
Axes of the slice: x: 4, y: 2, z: 32, core: 2. Of those that a mesh axis runs over, the one named last changes fastest.
The devices are a block of a 4x16x32 slice.
Arguments:
- queries: bfloat16 [64, 32, 32, 3072], P(('group', 'tm'), 'space', None, 'head'), parts along dimension 0, may hold values from -5.5 to 5.5
- keys: bfloat16 [64, 32, 32, 3072], P(('group', 'tm'), 'space', None, 'head'), parts along dimension 0, may hold values from -5.5 to 5.5
- values: bfloat16 [64, 32, 32, 3072], P(('group', 'tm'), 'space', None, 'head'), parts along dimension 0, may hold values from -6 to 6
- window: int32 [64, 4, 4, 27], P(('group', 'tm'), 'space'), parts along dimension 0, may hold values 0 or 1
Outputs:
- attended: bfloat16 [64, 32, 32, 3072], P(('group', 'tm'), 'space', None, 'head'), parts along dimension 0
There are 2 independent parts, one for each index of `group`. A program takes and returns all parts, laid end to end along the dimension named above; each array names one. Nothing has to cross between parts.
Inputs may be any that keep to these rules, and one draw needn't show every extreme that they name: `window`: slot dt * 9 + (dy + 1) * 3 + (dx + 1) of a query tile's entry enables the key tile dt frames earlier, dy tile rows and dx tile columns away; slot 4, the tile itself, is attended whatever it holds.
All inputs are finite; a program needn't handle non-finite values. No bound on the sum of `window` on one device may be relied on, other than what follows from the above.
Results may differ from a plain program's by a relative error of at most 0.0046.
Values may be sent and summed in bfloat16 or wider, within the bound.
No kernel may reach another device: no remote copies, remote signals or barrier semaphores. Data moves between devices by JAX's collectives and lax.ppermute only.
A program may use at most 128 MiB of HBM per device.

v0:
```python
import jax
import jax.numpy as jnp
from jax import lax
from jax.sharding import PartitionSpec as P

HDIM = 128
TILE = 8


def from_behind(block, axis, distance):
    devices = range(lax.axis_size(axis))
    route = [(i - distance, i) for i in devices if i - distance in devices]
    return lax.ppermute(block, axis, route)


def with_halo(value, sides, width):
    for axis, dim in sides:
        size, length = (lax.axis_size(axis), value.shape[dim])
        up = [(i, (i + 1) % size) for i in range(size - 1)]
        down = [(j, i) for i, j in up]
        last = lax.slice_in_dim(value, length - width, length, axis=dim)
        leading = lax.slice_in_dim(value, 0, width, axis=dim)
        before = lax.ppermute(last, axis, up)
        after = lax.ppermute(leading, axis, down)
        value = jnp.concatenate([before, value, after], axis=dim)
    return value


def on_device(queries, keys, values, window):
    channels = queries.shape[3]
    heads_here = channels // HDIM
    columns = queries.shape[2]
    tile_cols = columns // TILE
    frame_here = lax.axis_index("tm")
    row_here = lax.axis_index("space")
    row_count = lax.axis_size("space")
    paired = jnp.stack((keys[0], values[0]))
    earlier = from_behind(paired, "tm", 1)
    earliest = from_behind(paired, "tm", 2)
    frames = with_halo(jnp.stack((paired, earlier, earliest)), (("space", 2),), TILE)
    steps_back = jnp.arange(3, dtype=jnp.int32)
    frame_ok = steps_back <= frame_here
    row_ok = jnp.stack((row_here > 0, jnp.array(True), row_here < row_count - 1))
    slot_ids = jnp.arange(27, dtype=jnp.int32)
    slot_table = window[0, 0]
    score_scale = HDIM ** (-0.5)
    query_rows = queries[0]

    def attend(column):
        query_tile = lax.dynamic_slice_in_dim(query_rows, column * TILE, TILE, 1).reshape(
            TILE * TILE, heads_here, HDIM
        )
        lead_tile = jnp.clip(column - 1, 0, tile_cols - 3)
        key_block = lax.dynamic_slice_in_dim(frames, lead_tile * TILE, 3 * TILE, 3)
        key_rows = key_block[:, 0].reshape(27 * TILE * TILE, heads_here, HDIM)
        value_rows = key_block[:, 1].reshape(27 * TILE * TILE, heads_here, HDIM)
        offset = lead_tile + jnp.arange(3, dtype=jnp.int32) - column
        col_ok = jnp.abs(offset) <= 1
        slot_of = (
            steps_back[:, None, None] * 9
            + jnp.arange(3, dtype=jnp.int32)[None, :, None] * 3
            + jnp.clip(offset, -1, 1)[None, None, :]
            + 1
        )
        bits_row = lax.dynamic_index_in_dim(slot_table, column, 0, keepdims=False)
        picked = jnp.sum(jnp.where(slot_of[..., None] == slot_ids, bits_row, 0), axis=-1)
        allowed = (
            ((picked == 1) | (slot_of == 4))
            & frame_ok[:, None, None]
            & row_ok[None, :, None]
            & col_ok[None, None, :]
        )
        key_ok = jnp.broadcast_to(allowed[:, :, None, :, None], (3, 3, TILE, 3, TILE)).reshape(
            27 * TILE * TILE
        )
        scores = (
            jnp.einsum("qhd,khd->hqk", query_tile, key_rows, preferred_element_type=jnp.float32)
            * score_scale
        )
        scores = jnp.where(key_ok, scores, -jnp.inf)
        row_max = jnp.max(scores, axis=-1, keepdims=True)
        weights = jnp.exp(scores - row_max)
        row_sum = jnp.sum(weights, axis=-1)
        numerator = jnp.einsum(
            "hqk,khd->qhd",
            weights.astype(jnp.bfloat16),
            value_rows,
            preferred_element_type=jnp.float32,
        )
        result = numerator / row_sum.T[:, :, None]
        return result.astype(jnp.bfloat16).reshape(TILE, TILE, channels)

    per_tile = lax.map(attend, jnp.arange(tile_cols, dtype=jnp.int32))
    return per_tile.transpose(1, 0, 2, 3).reshape(1, TILE, columns, channels)


def solution(mesh):
    placed = (
        P(("group", "tm"), "space", None, "head"),
        P(("group", "tm"), "space", None, "head"),
        P(("group", "tm"), "space", None, "head"),
        P(("group", "tm"), "space", None, None),
    )
    return jax.shard_map(
        on_device,
        mesh=mesh,
        in_specs=placed,
        out_specs=P(("group", "tm"), "space", None, "head"),
        check_vma=False,
    )
```

profile of v0, /device:TPU:936, one launch (start us, length us, event | category | flops | bytes accessed | tf_op | source)
XLA Modules:
  0.0 463.1 jit_solution(824542814439964640)
XLA Ops:
  8.3 6.9 %collective-permute-start.1 = (bf16[2,8,32,1536]{3,2,1,0:T(8,128)(2,1)S(1)}, bf16[2,8,32,1536]{3,2,1,0:T(8,128)(2,1)S(1)}, u32[]{:S(2)}, u32[]{:S(2)}) collective-permute-start(bf16[2,8,32,1536]{3,2,1,0:T(8,128)(2,1)S(1)} %constant_dynamic-update-slice_fusion.1), channel_id=1, source_target_pairs={{0,16},{8,24},{16,32},{24,40},{32,48},{40,56},{48,64},{56,72},{64,... | collective-permute-start | bytes 4718600 | tf_op jit(solution)/shard_map/ppermute | solution.py:13
  15.3 59.0 %collective-permute-done = bf16[2,8,32,1536]{3,2,1,0:T(8,128)(2,1)S(1)} collective-permute-done((bf16[2,8,32,1536]{3,2,1,0:T(8,128)(2,1)S(1)}, bf16[2,8,32,1536]{3,2,1,0:T(8,128)(2,1)S(1)}, u32[]{:S(2)}, u32[]{:S(2)}) %collective-permute-start) | collective-permute-done | bytes 1572896 | tf_op jit(solution)/shard_map/ppermute | solution.py:13
  74.3 35.3 %collective-permute-done.1 = bf16[2,8,32,1536]{3,2,1,0:T(8,128)(2,1)S(1)} collective-permute-done((bf16[2,8,32,1536]{3,2,1,0:T(8,128)(2,1)S(1)}, bf16[2,8,32,1536]{3,2,1,0:T(8,128)(2,1)S(1)}, u32[]{:S(2)}, u32[]{:S(2)}) %collective-permute-start.1) | collective-permute-done | bytes 1572896 | tf_op jit(solution)/shard_map/ppermute | solution.py:13
  120.2 96.8 %collective-permute-done.2 = bf16[3,2,8,32,1536]{4,3,2,0,1:T(8,128)(2,1)} collective-permute-done((bf16[3,2,8,32,1536]{4,3,2,0,1:T(8,128)(2,1)}, bf16[3,2,8,32,1536]{4,3,2,0,1:T(8,128)(2,1)}, u32[]{:S(2)}, u32[]{:S(2)}) %collective-permute-start.2) | collective-permute-done | bytes 4718624 | tf_op jit(solution)/shard_map/ppermute | solution.py:23
  223.3 11.4 %pad_maximum_fusion = bf16[3,2,24,32,1536]{4,3,2,0,1:T(8,128)(2,1)} fusion(bf16[3,2,8,32,1536]{4,3,2,0,1:T(8,128)(2,1)} %collective-permute-done.3, bf16[1,2,8,32,1536]{4,3,2,0,1:T(8,128)(2,1)} %bitcast.47, bf16[1,2,8,32,1536]{4,3,2,0,1:T(8,128)(2,1)S(1)} %bitcast.45, bf16[1,2,8,32,1536]{4,3,2,0,1:T(8,128)(2,1)S(1)} %bitcast.43, ...), kind=kLoop, calls=%fused_computation.39 | loop fusion | flops 28311552 | bytes 28311552 | tf_op jit(solution)/shard_map/concatenate | solution.py:25
  234.7 226.3 %while.13 = (s32[]{:T(128)}, bf16[4,8,8,1536]{3,2,1,0:T(8,128)(2,1)}, s32[4]{0:T(128)S(1)}, bf16[3,2,24,32,1536]{4,3,2,0,1:T(8,128)(2,1)}, s32[4,27]{1,0:T(4,128...) while((s32[]{:T(128)}, ...), condition=%wide.region_4.5_spmd.clone, body=%wide.region_0.4_spmd.clone.sunk | while | flops 694272960 | bytes 92630008 | solution.py:93
  240.5 9.3 %constant_dynamic-slice_fusion.6 = (bf16[3,1,24,24,1536]{4,3,2,0,1:T(8,128)(2,1)}, bf16[3,1,24,24,1536]{4,3,2,0,1:T(8,128)(2,1)}) fusion(bf16[3,2,24,32,1536]{4,3,2,0,1:T(8,128)(2,1)} %get-tuple-element.274, s32[]{:T(128)S(6)} %select_n.66, s32[]{:T(128)S(6)} %add.188), kind=kLoop, calls=%fused_computation.24.clone.1 | loop fusion | bytes 21233672 | tf_op jit(solution)/shard_map/while/body/eval_jaxpr/slice | solution.py:55
  249.8 10.5 %squeeze.41 = bf16[1728,12,128]{2,1,0:T(8,128)(2,1)} reshape(bf16[3,1,24,24,1536]{4,3,2,0,1:T(8,128)(2,1)} %get-tuple-element.238) | data formatting | bytes 10616832 | tf_op jit(solution)/shard_map/while/body/eval_jaxpr/reshape;while/body/eval_jaxpr/squeeze | solution.py:55
  272.0 10.5 %squeeze.40 = bf16[1728,12,128]{2,1,0:T(8,128)(2,1)} reshape(bf16[3,1,24,24,1536]{4,3,2,0,1:T(8,128)(2,1)} %get-tuple-element.233) | data formatting | bytes 10616832 | tf_op jit(solution)/shard_map/while/body/eval_jaxpr/reshape;while/body/eval_jaxpr/squeeze | solution.py:56
  282.5 7.8 %fusion.52 = bf16[64,12,128]{2,0,1:T(8,128)(2,1)S(1)} fusion(bf16[1728,12,128]{2,1,0:T(8,128)(2,1)} %squeeze.40, f32[12,64,1728]{2,1,0:T(8,128)} %copy-done, f32[12,64]{1,0:T(8,128)S(1)} %get-tuple-element.240, pred[1728]{0:T(1024)(128)(4,1)S(1)} %reshape.94, f32[64,12]{0,1:T(8,128)S(1)} %bitcast.49), kind=kOutput, calls=%fused_computation.18.clone.1 | convolution fusion | flops 345243648 | bytes 10821312 | tf_op jit(solution)/shard_map/while/body/eval_jaxpr/hqk,khd->qhd/dot_general | solution.py:84
  297.1 9.3 %constant_dynamic-slice_fusion.6 = (bf16[3,1,24,24,1536]{4,3,2,0,1:T(8,128)(2,1)}, bf16[3,1,24,24,1536]{4,3,2,0,1:T(8,128)(2,1)}) fusion(bf16[3,2,24,32,1536]{4,3,2,0,1:T(8,128)(2,1)} %get-tuple-element.274, s32[]{:T(128)S(6)} %select_n.66, s32[]{:T(128)S(6)} %add.188), kind=kLoop, calls=%fused_computation.24.clone.1 | loop fusion | bytes 21233672 | tf_op jit(solution)/shard_map/while/body/eval_jaxpr/slice | solution.py:55
  306.4 10.5 %squeeze.41 = bf16[1728,12,128]{2,1,0:T(8,128)(2,1)} reshape(bf16[3,1,24,24,1536]{4,3,2,0,1:T(8,128)(2,1)} %get-tuple-element.238) | data formatting | bytes 10616832 | tf_op jit(solution)/shard_map/while/body/eval_jaxpr/reshape;while/body/eval_jaxpr/squeeze | solution.py:55
  318.6 6.3 %fusion.50 = (f32[12,64]{1,0:T(8,128)S(1)}, f32[12,64,1728]{2,1,0:T(8,128)S(1)}) fusion(pred[1728]{0:T(1024)(128)(4,1)S(1)} %reshape.94, bf16[1728,12,128]{2,1,0:T(8,128)(2,1)} %squeeze.41, bf16[64,12,128]{2,1,0:T(8,128)(2,1)S(1)} %reshape.95), kind=kOutput, calls=%fused_computation.9.clone.1 | convolution fusion | flops 343719168 | bytes 10818240 | tf_op jit(solution)/shard_map/while/body/eval_jaxpr/qhd,khd->hqk/dot_general | solution.py:77
  328.6 10.5 %squeeze.40 = bf16[1728,12,128]{2,1,0:T(8,128)(2,1)} reshape(bf16[3,1,24,24,1536]{4,3,2,0,1:T(8,128)(2,1)} %get-tuple-element.233) | data formatting | bytes 10616832 | tf_op jit(solution)/shard_map/while/body/eval_jaxpr/reshape;while/body/eval_jaxpr/squeeze | solution.py:56
  339.0 7.8 %fusion.52 = bf16[64,12,128]{2,0,1:T(8,128)(2,1)S(1)} fusion(bf16[1728,12,128]{2,1,0:T(8,128)(2,1)} %squeeze.40, f32[12,64,1728]{2,1,0:T(8,128)} %copy-done, f32[12,64]{1,0:T(8,128)S(1)} %get-tuple-element.240, pred[1728]{0:T(1024)(128)(4,1)S(1)} %reshape.94, f32[64,12]{0,1:T(8,128)S(1)} %bitcast.49), kind=kOutput, calls=%fused_computation.18.clone.1 | convolution fusion | flops 345243648 | bytes 10821312 | tf_op jit(solution)/shard_map/while/body/eval_jaxpr/hqk,khd->qhd/dot_general | solution.py:84
  353.6 9.3 %constant_dynamic-slice_fusion.6 = (bf16[3,1,24,24,1536]{4,3,2,0,1:T(8,128)(2,1)}, bf16[3,1,24,24,1536]{4,3,2,0,1:T(8,128)(2,1)}) fusion(bf16[3,2,24,32,1536]{4,3,2,0,1:T(8,128)(2,1)} %get-tuple-element.274, s32[]{:T(128)S(6)} %select_n.66, s32[]{:T(128)S(6)} %add.188), kind=kLoop, calls=%fused_computation.24.clone.1 | loop fusion | bytes 21233672 | tf_op jit(solution)/shard_map/while/body/eval_jaxpr/slice | solution.py:55
  363.0 10.5 %squeeze.41 = bf16[1728,12,128]{2,1,0:T(8,128)(2,1)} reshape(bf16[3,1,24,24,1536]{4,3,2,0,1:T(8,128)(2,1)} %get-tuple-element.238) | data formatting | bytes 10616832 | tf_op jit(solution)/shard_map/while/body/eval_jaxpr/reshape;while/body/eval_jaxpr/squeeze | solution.py:55
  385.2 10.5 %squeeze.40 = bf16[1728,12,128]{2,1,0:T(8,128)(2,1)} reshape(bf16[3,1,24,24,1536]{4,3,2,0,1:T(8,128)(2,1)} %get-tuple-element.233) | data formatting | bytes 10616832 | tf_op jit(solution)/shard_map/while/body/eval_jaxpr/reshape;while/body/eval_jaxpr/squeeze | solution.py:56
  395.6 7.8 %fusion.52 = bf16[64,12,128]{2,0,1:T(8,128)(2,1)S(1)} fusion(bf16[1728,12,128]{2,1,0:T(8,128)(2,1)} %squeeze.40, f32[12,64,1728]{2,1,0:T(8,128)} %copy-done, f32[12,64]{1,0:T(8,128)S(1)} %get-tuple-element.240, pred[1728]{0:T(1024)(128)(4,1)S(1)} %reshape.94, f32[64,12]{0,1:T(8,128)S(1)} %bitcast.49), kind=kOutput, calls=%fused_computation.18.clone.1 | convolution fusion | flops 345243648 | bytes 10821312 | tf_op jit(solution)/shard_map/while/body/eval_jaxpr/hqk,khd->qhd/dot_general | solution.py:84
  410.2 9.3 %constant_dynamic-slice_fusion.6 = (bf16[3,1,24,24,1536]{4,3,2,0,1:T(8,128)(2,1)}, bf16[3,1,24,24,1536]{4,3,2,0,1:T(8,128)(2,1)}) fusion(bf16[3,2,24,32,1536]{4,3,2,0,1:T(8,128)(2,1)} %get-tuple-element.274, s32[]{:T(128)S(6)} %select_n.66, s32[]{:T(128)S(6)} %add.188), kind=kLoop, calls=%fused_computation.24.clone.1 | loop fusion | bytes 21233672 | tf_op jit(solution)/shard_map/while/body/eval_jaxpr/slice | solution.py:55
  419.5 10.5 %squeeze.41 = bf16[1728,12,128]{2,1,0:T(8,128)(2,1)} reshape(bf16[3,1,24,24,1536]{4,3,2,0,1:T(8,128)(2,1)} %get-tuple-element.238) | data formatting | bytes 10616832 | tf_op jit(solution)/shard_map/while/body/eval_jaxpr/reshape;while/body/eval_jaxpr/squeeze | solution.py:55
  431.7 6.3 %fusion.50 = (f32[12,64]{1,0:T(8,128)S(1)}, f32[12,64,1728]{2,1,0:T(8,128)S(1)}) fusion(pred[1728]{0:T(1024)(128)(4,1)S(1)} %reshape.94, bf16[1728,12,128]{2,1,0:T(8,128)(2,1)} %squeeze.41, bf16[64,12,128]{2,1,0:T(8,128)(2,1)S(1)} %reshape.95), kind=kOutput, calls=%fused_computation.9.clone.1 | convolution fusion | flops 343719168 | bytes 10818240 | tf_op jit(solution)/shard_map/while/body/eval_jaxpr/qhd,khd->hqk/dot_general | solution.py:77
  441.7 10.5 %squeeze.40 = bf16[1728,12,128]{2,1,0:T(8,128)(2,1)} reshape(bf16[3,1,24,24,1536]{4,3,2,0,1:T(8,128)(2,1)} %get-tuple-element.233) | data formatting | bytes 10616832 | tf_op jit(solution)/shard_map/while/body/eval_jaxpr/reshape;while/body/eval_jaxpr/squeeze | solution.py:56
  452.2 7.8 %fusion.52 = bf16[64,12,128]{2,0,1:T(8,128)(2,1)S(1)} fusion(bf16[1728,12,128]{2,1,0:T(8,128)(2,1)} %squeeze.40, f32[12,64,1728]{2,1,0:T(8,128)} %copy-done, f32[12,64]{1,0:T(8,128)S(1)} %get-tuple-element.240, pred[1728]{0:T(1024)(128)(4,1)S(1)} %reshape.94, f32[64,12]{0,1:T(8,128)S(1)} %bitcast.49), kind=kOutput, calls=%fused_computation.18.clone.1 | convolution fusion | flops 345243648 | bytes 10821312 | tf_op jit(solution)/shard_map/while/body/eval_jaxpr/hqk,khd->qhd/dot_general | solution.py:84
  (91 shorter events, 76.0 us)
Async XLA Ops:
  2.4 71.8 %collective-permute-start = (bf16[2,8,32,1536]{3,2,1,0:T(8,128)(2,1)S(1)}, bf16[2,8,32,1536]{3,2,1,0:T(8,128)(2,1)S(1)}, u32[]{:S(2)}, u32[]{:S(2)}) collective-permute-start(bf16[2,8,32,1536]{3,2,1,0:T(8,128)(2,1)S(1)} %constant_dynamic-update-slice_fusion.1), channel_id=1, source_target_pairs={{0,8},{8,16},{16,24},{24,32},{32,40},{40,48},{48,56},{56,64},{64,7... | collective-permute-start | bytes 4718600 | tf_op jit(solution)/shard_map/ppermute | solution.py:13
  8.3 101.2 %collective-permute-start.1 = (bf16[2,8,32,1536]{3,2,1,0:T(8,128)(2,1)S(1)}, bf16[2,8,32,1536]{3,2,1,0:T(8,128)(2,1)S(1)}, u32[]{:S(2)}, u32[]{:S(2)}) collective-permute-start(bf16[2,8,32,1536]{3,2,1,0:T(8,128)(2,1)S(1)} %constant_dynamic-update-slice_fusion.1), channel_id=1, source_target_pairs={{0,16},{8,24},{16,32},{24,40},{32,48},{40,56},{48,64},{56,72},{64,... | collective-permute-start | bytes 4718600 | tf_op jit(solution)/shard_map/ppermute | solution.py:13
  109.6 1.1 copy-start.1
  113.1 103.9 %collective-permute-start.2 = (bf16[3,2,8,32,1536]{4,3,2,0,1:T(8,128)(2,1)}, bf16[3,2,8,32,1536]{4,3,2,0,1:T(8,128)(2,1)}, u32[]{:S(2)}, u32[]{:S(2)}) collective-permute-start(bf16[3,2,8,32,1536]{4,3,2,0,1:T(8,128)(2,1)} %pad_maximum_fusion.1), channel_id=1, source_target_pairs={{0,2},{2,4},{4,6},{1,3},{3,5},{5,7},{8,10},{10,12},{12,14},{9,11},... | collective-permute-start | bytes 14155784 | tf_op jit(solution)/shard_map/ppermute | solution.py:23
  118.8 104.5 %collective-permute-start.3 = (bf16[3,2,8,32,1536]{4,3,2,0,1:T(8,128)(2,1)}, bf16[3,2,8,32,1536]{4,3,2,0,1:T(8,128)(2,1)}, u32[]{:S(2)}, u32[]{:S(2)}) collective-permute-start(bf16[3,2,8,32,1536]{4,3,2,0,1:T(8,128)(2,1)} %pad_maximum_fusion.1), channel_id=1, source_target_pairs={{2,0},{4,2},{6,4},{3,1},{5,3},{7,5},{10,8},{12,10},{14,12},{11,9},... | collective-permute-start | bytes 14155784 | tf_op jit(solution)/shard_map/ppermute | solution.py:24
  268.4 2.4 copy-start
  324.9 2.4 copy-start
  381.5 2.4 copy-start
  438.1 2.4 copy-start
where the time goes:
time: 466 us; the launch traced here: 463 us
  waiting for transfers between devices  197 us (42%)
  local copies, waits for them, and re-layouts  151 us (32%)
  matrix products  56.6 us (12%)
  other arithmetic  25.8 us (6%)
  starting transfers between devices  19.9 us (4%)
  loops' own time  12.6 us (3%)
    ppermute x1, waiting for transfers between devices, with_halo(): before = lax.ppermute(last, axis, up)  96.8 us
    ppermute x2, waiting for transfers between devices, from_behind(): return lax.ppermute(block, axis, route)  94.3 us
    squeeze x4, local copies, waits for them, and re-layouts, attend(): value_rows = key_block[:, 1].reshape(27 * TILE * TILE, heads_here, HDIM)  41.8 us
    squeeze x4, local copies, waits for them, and re-layouts, attend(): key_rows = key_block[:, 0].reshape(27 * TILE * TILE, heads_here, HDIM)  41.8 us
    slice x4, local copies, waits for them, and re-layouts, attend(): key_rows = key_block[:, 0].reshape(27 * TILE * TILE, heads_here, HDIM)  37.3 us
    dot_general x4, matrix products, attend(): jnp.einsum('hqk,khd->qhd', weights.astype(jnp.bfloat16), value_rows, pref...  31.2 us
    dot_general x4, matrix products, attend(): jnp.einsum('qhd,khd->hqk', query_tile, key_rows, preferred_element_type=j...  25.4 us
    ppermute x2, starting transfers between devices, from_behind(): return lax.ppermute(block, axis, route)  12.9 us
  transfers between devices with their start and end apart: 4, of which 4 were waited for; matrix products, arithmetic and copies ran while one was open for 0% of the time, Pallas kernels for 0%

commit v1 on v0

v1 whole, which is shorter than its diff:
```python
import functools

import jax
import jax.numpy as jnp
from jax import lax
from jax.experimental import pallas as pl
from jax.experimental.pallas import tpu as pltpu
from jax.sharding import PartitionSpec as P


HDIM = 128
TILE = 8
SLOTS = 27
MASKS = 48
STATS = 8
NEVER = -1e30
FLOOR = -1e25
SCALE = (HDIM**-0.5) * 1.4426950408889634
WHOLE = pl.BlockSpec(memory_space=pltpu.VMEM)
ROW_BEFORE, ROW_AFTER, FRAME_1, FRAME_2 = range(4)
LAG = 6


def shift(block, axis, by, skip=0, ahead=0):
    size = lax.axis_size(axis)
    route = [
        (i, i + by)
        for i in range(skip, size)
        if 0 <= i + by < size and i + by + ahead < size and i + ahead < size
    ]
    return lax.ppermute(block, axis, route)


def masks(tcols, flags, window):
    row = lax.broadcasted_iota(jnp.int32, (MASKS, HDIM), 0)
    lane = lax.broadcasted_iota(jnp.int32, (MASKS, HDIM), 1)
    place, key_tile = lax.div(row, tcols), lax.rem(row, tcols)
    total = jnp.zeros((MASKS, HDIM), jnp.float32)
    for c in range(tcols):
        bits = jnp.broadcast_to(window[c : c + 1, :], (MASKS, SLOTS))
        bits = jnp.concatenate([bits, jnp.zeros((MASKS, HDIM - SLOTS), jnp.float32)], axis=1)
        step = key_tile - c
        bits = jnp.where((lane == place * 3 + step + 1) & (jnp.abs(step) <= 1), bits, 0.0)
        total = jnp.where(lane == c, jnp.sum(bits, axis=1, keepdims=True), total)
    own = (place == 1) & (key_tile == lane)
    back, dy = lax.div(place, 3), lax.rem(place, 3)
    ok = jnp.full((MASKS, HDIM), 1, jnp.int32)
    ok = jnp.where(dy == 0, flags[ROW_BEFORE], ok)
    ok = jnp.where(dy == 2, flags[ROW_AFTER], ok)
    ok = jnp.where(back == 1, ok * flags[FRAME_1], ok)
    ok = jnp.where(back == 2, ok * flags[FRAME_2], ok)
    allowed = ((total > 0.5) | own) & (ok > 0)
    return jnp.where(allowed | (lane >= tcols), 0.0, NEVER).astype(jnp.bfloat16)


def pack_kernel(heads, tokens, q_ref, k_ref, v_ref, w_ref, *refs):
    packed, ok_ref, (vbuf, wbuf, sems) = refs[:4], refs[4], refs[5:]
    table = pltpu.make_async_copy(w_ref.at[0, 0], wbuf, sems.at[6 * heads])
    table.start()
    rows, cols = q_ref.shape[1], q_ref.shape[2]
    copies = {}
    for half in range(2):
        qc_ref, kv_ref = packed[2 * half : 2 * half + 2]
        for j in range(heads):
            head = half * heads + j
            lanes = pl.ds(head * HDIM, HDIM)
            at = pl.ds(j * tokens, tokens)
            slot = pl.ds(head * tokens, tokens)
            for n, (src, dst) in enumerate(
                ((v_ref, vbuf.at[slot]), (k_ref, kv_ref.at[at]), (q_ref, qc_ref.at[at]))
            ):
                copy = pltpu.make_async_copy(
                    src.at[0, :, :, lanes],
                    dst.reshape(rows, cols, HDIM),
                    sems.at[3 * head + n],
                )
                copy.start()
                copies[half, j, n] = copy
    here, frame = lax.axis_index("space"), lax.axis_index("tm")
    tests = here > 0, here < lax.axis_size("space") - 1, frame > 0, frame > 1
    flags = [jnp.where(test, 1, 0) for test in tests]
    sub = lax.broadcasted_iota(jnp.int32, ok_ref.shape, 0)
    ok = jnp.zeros(ok_ref.shape, jnp.int32)
    for n, flag in enumerate(flags):
        ok = jnp.where(sub == n, flag, ok)
    ok_ref[...] = ok
    table.wait()
    mask = masks(cols // TILE, flags, wbuf[...].astype(jnp.float32))
    for half in range(2):
        qc_ref, kv_ref = packed[2 * half : 2 * half + 2]
        qc_ref[heads * tokens :, :] = mask
        for j in range(heads):
            copies[half, j, 0].wait()
            slot = (half * heads + j) * tokens
            vt = vbuf[slot : slot + tokens, :].T
            base = (heads + j) * tokens
            for s in range(tokens // HDIM):
                kv_ref[base + s * HDIM : base + (s + 1) * HDIM, :] = vt[
                    :, s * HDIM : (s + 1) * HDIM
                ]
    for half in range(2):
        for j in range(heads):
            copies[half, j, 1].wait()
            copies[half, j, 2].wait()


def pack(heads, queries, keys, values, window):
    tokens = queries.shape[1] * queries.shape[2]
    shapes = [
        jax.ShapeDtypeStruct((heads * tokens + MASKS, HDIM), jnp.bfloat16),
        jax.ShapeDtypeStruct((2 * heads * tokens, HDIM), jnp.bfloat16),
    ]
    return pl.pallas_call(
        functools.partial(pack_kernel, heads, tokens),
        out_shape=shapes * 2 + [jax.ShapeDtypeStruct((STATS, HDIM), jnp.int32)],
        in_specs=[pl.BlockSpec(memory_space=pltpu.HBM)] * 4,
        out_specs=[WHOLE] * 5,
        scratch_shapes=[
            pltpu.VMEM((2 * heads * tokens, HDIM), jnp.bfloat16),
            pltpu.VMEM(window.shape[2:], window.dtype),
            pltpu.SemaphoreType.DMA((6 * heads + 1,)),
        ],
        compiler_params=pltpu.CompilerParams(vmem_limit_bytes=8 * 2**20),
        cost_estimate=pl.CostEstimate(
            flops=10**9, bytes_accessed=12 * heads * tokens * HDIM, transcendentals=0
        ),
        name="pack",
    )(queries, keys, values, window)


def side_by_side(ref, base, tokens):
    return jnp.concatenate(
        [ref[base + s * HDIM : base + (s + 1) * HDIM, :] for s in range(tokens // HDIM)], axis=1
    )


def write_partial(out_ref, heads, tokens, outs, lse):
    halves = tokens // HDIM
    for j, out in outs:
        for s in range(halves):
            at = j * tokens + s * HDIM
            out_ref[at : at + HDIM, :] = out[:, s * HDIM : (s + 1) * HDIM]
    if lse is not None:
        for p in range(3):
            part = lse.astype(jnp.bfloat16)
            lse = lse - part.astype(jnp.float32)
            for s in range(halves):
                at = heads * tokens + (p * halves + s) * STATS
                out_ref[at : at + STATS, :] = part[:, s * HDIM : (s + 1) * HDIM]


def read_lse(in_ref, heads, tokens):
    halves = tokens // HDIM
    parts = []
    for s in range(halves):
        part = jnp.zeros((STATS, HDIM), jnp.float32)
        for p in range(3):
            at = heads * tokens + (p * halves + s) * STATS
            part = part + in_ref[at : at + STATS, :].astype(jnp.float32)
        parts.append(part)
    return jnp.concatenate(parts, axis=1)


def attend_kernel(heads, tokens, cols, sets, packed, *refs):
    q_refs, refs = refs[: len(sets)], refs[len(sets) :]
    blocks = len(sets[0])
    kvs, refs = refs[:blocks], refs[blocks:]
    tcols = cols // TILE
    repeat = tokens // cols

    row = lax.broadcasted_iota(jnp.int32, (cols, HDIM), 0)
    lane = lax.broadcasted_iota(jnp.int32, (cols, HDIM), 1)
    tile = jnp.where(lane == lax.div(row, TILE), 1.0, 0.0).astype(jnp.bfloat16)
    tile = jnp.concatenate([tile] * repeat, axis=0)
    bias = {}
    for which, places in enumerate(sets):
        rows = q_refs[which][heads * tokens :, :].astype(jnp.float32)
        for n, place in enumerate(places):
            part = [
                jnp.broadcast_to(rows[place * tcols + c : place * tcols + c + 1, :], (TILE, HDIM))
                for c in range(tcols)
            ]
            part = jnp.concatenate(part, axis=0).astype(jnp.bfloat16)
            bias[which, n] = jnp.concatenate([part] * repeat, axis=0)

    streams = [(which, j) for which in range(len(sets)) for j in range(heads)]
    group = 3 if len(streams) % 3 == 0 else 1
    units = [
        (n, stream)
        for base in range(0, len(streams), group)
        for n in range(blocks)
        for stream in streams[base : base + group]
    ]
    tops, totals, outs, ready = {}, {}, {}, {}
    sub = lax.broadcasted_iota(jnp.int32, (STATS, tokens), 0)
    lses = [jnp.full((STATS, tokens), NEVER, jnp.float32) for _ in sets]
    for i in range(len(units) + LAG):
        if i < len(units):
            n, key = units[i]
            which, j = key
            at = slice(j * tokens, (j + 1) * tokens)
            qcat = jnp.concatenate([q_refs[which][at, :], tile], axis=1)
            kcat = jnp.concatenate([kvs[n][at, :], bias[which, n]], axis=1)
            scores = lax.dot_general(
                kcat, qcat, (((1,), (1,)), ((), ())), preferred_element_type=jnp.float32
            )
            top = jnp.max(scores, axis=0, keepdims=True) * SCALE
            old = tops.get(key)
            top = jnp.maximum(top, FLOOR if old is None else old)
            tops[key] = top
            weights = jnp.exp2(scores * SCALE - top)
            total = jnp.sum(weights, axis=0, keepdims=True)
            fade = None if old is None else jnp.exp2(old - top)
            totals[key] = total if old is None else totals[key] * fade + total
            ready[i] = fade, weights.astype(jnp.bfloat16)
        if i >= LAG:
            n, key = units[i - LAG]
            which, j = key
            fade, weights = ready.pop(i - LAG)
            out = jnp.dot(
                side_by_side(kvs[n], (heads + j) * tokens, tokens),
                weights,
                preferred_element_type=jnp.float32,
            )
            outs[key] = out if fade is None else outs[key] * fade + out
            if n == blocks - 1:
                total = totals[key]
                out = outs.pop(key) * (1.0 / jnp.maximum(total, 1e-30))
                lse = tops[key] + jnp.log2(total)
                lses[which] = jnp.where((sub == j) & (total > 0), lse, lses[which])
                if packed[which]:
                    write_partial(
                        refs[which], heads, tokens, [(j, out.astype(jnp.bfloat16))], None
                    )
                else:
                    refs[which][j * HDIM : (j + 1) * HDIM, :] = out
    for which, lse in enumerate(lses):
        if packed[which]:
            write_partial(refs[which], heads, tokens, [], lse)
        else:
            refs[which][heads * HDIM :, :] = lse


def partial_shape(heads, tokens):
    stats = 3 * (tokens // HDIM) * STATS
    return jax.ShapeDtypeStruct((heads * tokens + stats, HDIM), jnp.bfloat16)


def attend(sets, packed, heads, shape, qs, kvs):
    rows, cols, _ = shape
    tokens = rows * cols
    out_shape = [
        partial_shape(heads, tokens)
        if p
        else jax.ShapeDtypeStruct((heads * HDIM + STATS, tokens), jnp.float32)
        for p in packed
    ]
    return pl.pallas_call(
        functools.partial(attend_kernel, heads, tokens, cols, sets, packed),
        out_shape=out_shape,
        in_specs=[WHOLE] * (len(qs) + len(kvs)),
        out_specs=[WHOLE] * len(packed),
        compiler_params=pltpu.CompilerParams(vmem_limit_bytes=16 * 2**20),
        cost_estimate=pl.CostEstimate(
            flops=10**9, bytes_accessed=8 * heads * tokens * HDIM, transcendentals=0
        ),
        name="attend",
    )(*qs, *kvs)


def merged(heads, tokens, ok_ref, local, priors, checks, write):
    lses = [local[heads * HDIM :, :]]
    for ref, flag in zip(priors, checks):
        ok = jnp.concatenate([ok_ref[flag : flag + 1, :]] * (tokens // HDIM), axis=1)
        lses.append(jnp.where(ok > 0, read_lse(ref, heads, tokens), NEVER))
    top = functools.reduce(jnp.maximum, lses)
    shares = [jnp.exp2(lse - top) for lse in lses]
    total = functools.reduce(jnp.add, shares)
    shares = [share * (1.0 / total) for share in shares]
    for j in range(heads):
        out = local[j * HDIM : (j + 1) * HDIM, :] * shares[0][j : j + 1, :]
        for ref, share in zip(priors, shares[1:]):
            piece = side_by_side(ref, j * tokens, tokens).astype(jnp.float32)
            out = out + piece * share[j : j + 1, :]
        write(j, out.astype(jnp.bfloat16))
    return jnp.where(top > 0.5 * NEVER, top + jnp.log2(total), NEVER)


def merge_kernel(heads, tokens, checks, ok_ref, local, *refs):
    priors, out_ref = refs[:-1], refs[-1]

    def write(j, out):
        write_partial(out_ref, heads, tokens, [(j, out)], None)

    lse = merged(heads, tokens, ok_ref, local, priors, checks, write)
    write_partial(out_ref, heads, tokens, [], lse)


def finish_kernel(heads, tokens, cols, parts, ok_ref, *refs):
    out_ref, stage, sems = refs[-3:]
    copies = []
    for first, checks in parts:
        local, priors, refs = refs[0], refs[1 : 1 + len(checks)], refs[1 + len(checks) :]

        def write(j, out):
            at = pl.ds((first + j) * tokens, tokens)
            stage[at, :] = out.T
            copy = pltpu.make_async_copy(
                stage.at[at].reshape(tokens // cols, cols, HDIM),
                out_ref.at[0, :, :, pl.ds((first + j) * HDIM, HDIM)],
                sems.at[first + j],
            )
            copy.start()
            copies.append(copy)

        merged(heads, tokens, ok_ref, local, priors, checks, write)
    for copy in copies:
        copy.wait()


def merge(heads, shape, ok, local, priors, checks):
    tokens = shape[0] * shape[1]
    return pl.pallas_call(
        functools.partial(merge_kernel, heads, tokens, checks),
        out_shape=partial_shape(heads, tokens),
        in_specs=[WHOLE] * (2 + len(priors)),
        out_specs=WHOLE,
        compiler_params=pltpu.CompilerParams(vmem_limit_bytes=8 * 2**20),
        cost_estimate=pl.CostEstimate(
            flops=10**8, bytes_accessed=8 * heads * tokens * HDIM, transcendentals=0
        ),
        name="merge",
    )(ok, local, *priors)


def finish(heads, shape, ok, *parts):
    rows, cols, channels = shape
    tokens = rows * cols
    args = [ok]
    for _, local, priors, _ in parts:
        args += [local, *priors]
    layout = tuple((first, checks) for first, _, _, checks in parts)
    return pl.pallas_call(
        functools.partial(finish_kernel, heads, tokens, cols, layout),
        out_shape=jax.ShapeDtypeStruct((1, rows, cols, channels), jnp.bfloat16),
        in_specs=[WHOLE] * len(args),
        out_specs=pl.BlockSpec(memory_space=pl.ANY),
        scratch_shapes=[
            pltpu.VMEM((tokens * channels // HDIM, HDIM), jnp.bfloat16),
            pltpu.SemaphoreType.DMA((channels // HDIM,)),
        ],
        compiler_params=pltpu.CompilerParams(vmem_limit_bytes=8 * 2**20),
        cost_estimate=pl.CostEstimate(
            flops=10**8, bytes_accessed=16 * heads * tokens * HDIM, transcendentals=0
        ),
        name="finish",
    )(*args)


def steps(queries, keys, values, window):
    _, rows, cols, channels = queries.shape
    args = (
        pltpu.with_memory_space_constraint(a, pltpu.HBM) for a in (queries, keys, values, window)
    )
    half = channels // HDIM // 2
    shape = (rows, cols, channels)
    go = functools.partial(attend, heads=half, shape=shape)
    qa, kva, qb, kvb, ok = pack(half, *args)

    a1 = shift(kva, "tm", 1)
    a2 = shift(a1, "tm", 1, skip=1)
    qm = shift(qa, "space", 1)
    qp = shift(qa, "space", -1)
    along = (kva, a1, a2)
    frames = [tuple(3 * back + dy for back in range(3)) for dy in range(3)]
    both, mine = (True, True), (False,)
    km, kp = go((frames[2], frames[0]), both, qs=(qm, qp), kvs=along)
    pp = shift(km, "space", -1)
    pm = shift(kp, "space", 1)
    (ka,) = go((frames[1],), mine, qs=(qa,), kvs=along)

    q1 = shift(qb, "tm", -1)
    q2 = shift(q1, "tm", -1, ahead=1)
    lo = shift(kvb, "space", 1)
    hi = shift(kvb, "space", -1)
    across = (lo, kvb, hi)
    offsets = [tuple(3 * back + dy for dy in range(3)) for back in range(3)]

    (k2,) = go((offsets[2],), (True,), qs=(q2,), kvs=across)
    p2 = shift(k2, "tm", 1, ahead=1)
    k1, k0 = go((offsets[1], offsets[0]), (False, False), qs=(q1, qb), kvs=across)
    m1 = merge(half, shape, ok, k1, (p2,), (FRAME_1,))
    p1 = shift(m1, "tm", 1)

    part_a = (0, ka, (pm, pp), (ROW_BEFORE, ROW_AFTER))
    part_b = (half, k0, (p1,), (FRAME_1,))
    return finish(half, shape, ok, part_a, part_b)


def solution(mesh):
    arrays = P(("group", "tm"), "space", None, "head")
    return jax.shard_map(
        steps,
        mesh=mesh,
        in_specs=(arrays, arrays, arrays, P(("group", "tm"), "space", None, None)),
        out_specs=arrays,
        check_vma=False,
    )
```

time: 466 us -> 95.4 us (0.20)
  the two profiles are of different devices: /device:TPU:936 before, /device:TPU:160 now
where the time goes in v1:
time: 95.4 us; the launch traced here: 94.9 us
  starting transfers between devices  65.3 us (68%)
  waiting for transfers between devices  15.7 us (16%)
  Pallas kernels  13.8 us (14%)
    ppermute x12, starting transfers between devices, shift(): return lax.ppermute(block, axis, route)  65.3 us
    ppermute x12, waiting for transfers between devices, shift(): return lax.ppermute(block, axis, route)  15.7 us
    pallas_call x4, Pallas kernels, attend(): pl.pallas_call(functools.partial(attend_kernel, heads, tokens, cols, sets...  10.3 us
    pallas_call x1, Pallas kernels, pack(): pl.pallas_call(functools.partial(pack_kernel, heads, tokens), out_shape=s...  2.16 us
  transfers between devices with their start and end apart: 12, of which 6 were waited for; matrix products, arithmetic and copies ran while one was open for 0% of the time, Pallas kernels for 11%

profile of v1, /device:TPU:160, one launch (start us, length us, event | category | flops | bytes accessed | tf_op | source)
XLA Modules:
  0.0 94.9 jit_solution(15736185877498314428)
XLA Ops:
  0.0 2.2 %pack.1 = (bf16[1584,128]{1,0:T(8,128)(2,1)S(1)}, bf16[3072,128]{1,0:T(8,128)(2,1)S(1)}, bf16[1584,128]{1,0:T(8,128)(2,1)S(1)}, bf16[3072,128]{1,0:T(8,128)(2,1)S(1)}, s32[8,128]{1,0:T(8,128)S(1)}) custom-call(bf16[1,8,32,1536]{3,2,1,0:T(8,128)(2,1)} %q_ref.1, bf16[1,8,32,1536]{3,2,1,0:T(8,128)(2,1)} %k_ref.1, bf16[1,8,32,1536]{3,2,1,0:T(8,128)(2,1)} %v_ref.1, ...), custom_call_target="tpu_custom_call" | custom-call | flops 1000000000 | bytes 2359296 | tf_op jit(solution)/shard_map/pack/pallas_call | solution.py:113
  2.2 4.7 %collective-permute-start = (bf16[3072,128]{1,0:T(8,128)(2,1)S(1)}, bf16[3072,128]{1,0:T(8,128)(2,1)S(1)}, u32[]{:S(2)}, u32[]{:S(2)}) collective-permute-start(bf16[3072,128]{1,0:T(8,128)(2,1)S(1)} %get-tuple-element.16.refs_1_.refs_2_), channel_id=1, source_target_pairs={{0,8},{8,16},{16,24},{24,32},{32,40},{40,48},{48,56},{56,64},{64,7... | collective-permute-start | bytes 2359304 | tf_op jit(solution)/shard_map/ppermute | solution.py:31
  6.9 37.8 %collective-permute-start.6 = (bf16[1584,128]{1,0:T(8,128)(2,1)S(1)}, bf16[1584,128]{1,0:T(8,128)(2,1)S(1)}, u32[]{:S(2)}, u32[]{:S(2)}) collective-permute-start(bf16[1584,128]{1,0:T(8,128)(2,1)S(1)} %get-tuple-element.19.refs_1_), channel_id=1, source_target_pairs={{8,0},{16,8},{24,16},{32,24},{40,32},{48,40},{56,48},{64,56},{72,6... | collective-permute-start | bytes 1216520 | tf_op jit(solution)/shard_map/ppermute | solution.py:31
  44.7 1.4 %collective-permute-start.7 = (bf16[3072,128]{1,0:T(8,128)(2,1)S(1)}, bf16[3072,128]{1,0:T(8,128)(2,1)S(1)}, u32[]{:S(2)}, u32[]{:S(2)}) collective-permute-start(bf16[3072,128]{1,0:T(8,128)(2,1)S(1)} %get-tuple-element.20.refs_3_.refs_2_), channel_id=1, source_target_pairs={{0,2},{2,4},{4,6},{1,3},{3,5},{5,7},{8,10},{10,12},{12,14},{9,11},... | collective-permute-start | bytes 2359304 | tf_op jit(solution)/shard_map/ppermute | solution.py:31
  46.1 1.3 %collective-permute-start.8 = (bf16[3072,128]{1,0:T(8,128)(2,1)S(1)}, bf16[3072,128]{1,0:T(8,128)(2,1)S(1)}, u32[]{:S(2)}, u32[]{:S(2)}) collective-permute-start(bf16[3072,128]{1,0:T(8,128)(2,1)S(1)} %get-tuple-element.20.refs_3_.refs_2_), channel_id=1, source_target_pairs={{2,0},{4,2},{6,4},{3,1},{5,3},{7,5},{10,8},{12,10},{14,12},{11,9},... | collective-permute-start | bytes 2359304 | tf_op jit(solution)/shard_map/ppermute | solution.py:31
  47.4 2.7 %collective-permute-done.6.refs_0_ = bf16[1584,128]{1,0:T(8,128)(2,1)S(1)} collective-permute-done((bf16[1584,128]{1,0:T(8,128)(2,1)S(1)}, bf16[1584,128]{1,0:T(8,128)(2,1)S(1)}, u32[]{:S(2)}, u32[]{:S(2)}) %collective-permute-start.6) | collective-permute-done | bytes 405536 | tf_op jit(solution)/shard_map/ppermute | solution.py:31
  50.1 4.4 %collective-permute-start.9 = (bf16[1584,128]{1,0:T(8,128)(2,1)S(1)}, bf16[1584,128]{1,0:T(8,128)(2,1)S(1)}, u32[]{:S(2)}, u32[]{:S(2)}) collective-permute-start(bf16[1584,128]{1,0:T(8,128)(2,1)S(1)} %collective-permute-done.6.refs_0_), channel_id=1, source_target_pairs={{8,0},{16,8},{24,16},{32,24},{40,32},{48,40},{56,48},{64,56},{72,6... | collective-permute-start | bytes 1216520 | tf_op jit(solution)/shard_map/ppermute | solution.py:31
  54.6 1.5 %collective-permute-start.1 = (bf16[3072,128]{1,0:T(8,128)(2,1)S(1)}, bf16[3072,128]{1,0:T(8,128)(2,1)S(1)}, u32[]{:S(2)}, u32[]{:S(2)}) collective-permute-start(bf16[3072,128]{1,0:T(8,128)(2,1)S(1)} %collective-permute-done.refs_2_.refs_3_), channel_id=1, source_target_pairs={{8,16},{16,24},{24,32},{32,40},{40,48},{48,56},{56,64},{64,72},{72... | collective-permute-start | bytes 2359304 | tf_op jit(solution)/shard_map/ppermute | solution.py:31
  56.1 4.1 %collective-permute-done.8.refs_4_.refs_3_ = bf16[3072,128]{1,0:T(8,128)(2,1)S(1)} collective-permute-done((bf16[3072,128]{1,0:T(8,128)(2,1)S(1)}, bf16[3072,128]{1,0:T(8,128)(2,1)S(1)}, u32[]{:S(2)}, u32[]{:S(2)}) %collective-permute-start.8) | collective-permute-done | bytes 786464 | tf_op jit(solution)/shard_map/ppermute | solution.py:31
  60.2 1.8 %attend.7 = bf16[1584,128]{1,0:T(8,128)(2,1)S(1)} custom-call(bf16[1584,128]{1,0:T(8,128)(2,1)S(1)} %collective-permute-done.9.refs_0_, bf16[3072,128]{1,0:T(8,128)(2,1)S(1)} %collective-permute-done.7.refs_2_.refs_1_, bf16[3072,128]{1,0:T(8,128)(2,1)S(1)} %get-tuple-element.20.refs_3_.refs_2_, bf16[3072,128]{1,0:T(8,128)(2,1)S(1)} %collective-permute-done.8.refs_4_.refs_3_), custom_call_target="tpu_custom_call" | custom-call | flops 1000000000 | bytes 1572864 | tf_op jit(solution)/shard_map/attend/pallas_call | solution.py:258
  62.1 1.9 %collective-permute-start.10 = (bf16[1584,128]{1,0:T(8,128)(2,1)S(1)}, bf16[1584,128]{1,0:T(8,128)(2,1)S(1)}, u32[]{:S(2)}, u32[]{:S(2)}) collective-permute-start(bf16[1584,128]{1,0:T(8,128)(2,1)S(1)} %attend.7), channel_id=1, source_target_pairs={{0,8},{8,16},{16,24},{24,32},{32,40},{40,48},{48,56},{56,64},{64,7... | collective-permute-start | bytes 1216520 | tf_op jit(solution)/shard_map/ppermute | solution.py:31
  64.0 1.6 %collective-permute-start.2 = (bf16[1584,128]{1,0:T(8,128)(2,1)S(1)}, bf16[1584,128]{1,0:T(8,128)(2,1)S(1)}, u32[]{:S(2)}, u32[]{:S(2)}) collective-permute-start(bf16[1584,128]{1,0:T(8,128)(2,1)S(1)} %get-tuple-element.15.refs_0_), channel_id=1, source_target_pairs={{0,2},{2,4},{4,6},{1,3},{3,5},{5,7},{8,10},{10,12},{12,14},{9,11},... | collective-permute-start | bytes 1216520 | tf_op jit(solution)/shard_map/ppermute | solution.py:31
  65.7 1.3 %collective-permute-start.3 = (bf16[1584,128]{1,0:T(8,128)(2,1)S(1)}, bf16[1584,128]{1,0:T(8,128)(2,1)S(1)}, u32[]{:S(2)}, u32[]{:S(2)}) collective-permute-start(bf16[1584,128]{1,0:T(8,128)(2,1)S(1)} %get-tuple-element.15.refs_0_), channel_id=1, source_target_pairs={{2,0},{4,2},{6,4},{3,1},{5,3},{7,5},{10,8},{12,10},{14,12},{11,9},... | collective-permute-start | bytes 1216520 | tf_op jit(solution)/shard_map/ppermute | solution.py:31
  67.0 3.3 %attend.6 = (f32[776,256]{1,0:T(8,128)S(1)}, f32[776,256]{1,0:T(8,128)S(1)}) custom-call(bf16[1584,128]{1,0:T(8,128)(2,1)S(1)} %collective-permute-done.6.refs_0_, bf16[1584,128]{1,0:T(8,128)(2,1)S(1)} %get-tuple-element.19.refs_1_, bf16[3072,128]{1,0:T(8,128)(2,1)S(1)} %collective-permute-done.7.refs_2_.refs_1_, ...), custom_call_target="tpu_custom_call" | custom-call | flops 1000000000 | bytes 1572864 | tf_op jit(solution)/shard_map/attend/pallas_call | solution.py:258
  70.3 1.6 %collective-permute-done.10.refs_0_ = bf16[1584,128]{1,0:T(8,128)(2,1)S(1)} collective-permute-done((bf16[1584,128]{1,0:T(8,128)(2,1)S(1)}, bf16[1584,128]{1,0:T(8,128)(2,1)S(1)}, u32[]{:S(2)}, u32[]{:S(2)}) %collective-permute-start.10) | collective-permute-done | bytes 405536 | tf_op jit(solution)/shard_map/ppermute | solution.py:31
  72.1 4.3 %collective-permute-start.11 = (bf16[1584,128]{1,0:T(8,128)(2,1)S(1)}, bf16[1584,128]{1,0:T(8,128)(2,1)S(1)}, u32[]{:S(2)}, u32[]{:S(2)}) collective-permute-start(bf16[1584,128]{1,0:T(8,128)(2,1)S(1)} %merge.1), channel_id=1, source_target_pairs={{0,8},{8,16},{16,24},{24,32},{32,40},{40,48},{48,56},{56,64},{64,7... | collective-permute-start | bytes 1216520 | tf_op jit(solution)/shard_map/ppermute | solution.py:31
  76.3 0.5 collective-permute-done.3.refs_1_
  76.9 3.3 %attend.5 = (bf16[1584,128]{1,0:T(8,128)(2,1)S(1)}, bf16[1584,128]{1,0:T(8,128)(2,1)S(1)}) custom-call(bf16[1584,128]{1,0:T(8,128)(2,1)S(1)} %collective-permute-done.2.refs_0_, bf16[1584,128]{1,0:T(8,128)(2,1)S(1)} %collective-permute-done.3.refs_1_, bf16[3072,128]{1,0:T(8,128)(2,1)S(1)} %get-tuple-element.16.refs_1_.refs_2_, ...), custom_call_target="tpu_custom_call" | custom-call | flops 1000000000 | bytes 1572864 | tf_op jit(solution)/shard_map/attend/pallas_call | solution.py:258
  80.2 3.7 %collective-permute-start.4 = (bf16[1584,128]{1,0:T(8,128)(2,1)S(1)}, bf16[1584,128]{1,0:T(8,128)(2,1)S(1)}, u32[]{:S(2)}, u32[]{:S(2)}) collective-permute-start(bf16[1584,128]{1,0:T(8,128)(2,1)S(1)} %get-tuple-element.17), channel_id=1, source_target_pairs={{0,2},{2,4},{4,6},{1,3},{3,5},{5,7},{8,10},{10,12},{12,14},{9,11},... | collective-permute-start | bytes 1216520 | tf_op jit(solution)/shard_map/ppermute | solution.py:31
  83.9 1.3 %collective-permute-start.5 = (bf16[1584,128]{1,0:T(8,128)(2,1)S(1)}, bf16[1584,128]{1,0:T(8,128)(2,1)S(1)}, u32[]{:S(2)}, u32[]{:S(2)}) collective-permute-start(bf16[1584,128]{1,0:T(8,128)(2,1)S(1)} %get-tuple-element.18), channel_id=1, source_target_pairs={{2,0},{4,2},{6,4},{3,1},{5,3},{7,5},{10,8},{12,10},{14,12},{11,9},... | collective-permute-start | bytes 1216520 | tf_op jit(solution)/shard_map/ppermute | solution.py:31
  85.2 1.8 %attend.4.refs_0_ = f32[776,256]{1,0:T(8,128)S(1)} custom-call(bf16[1584,128]{1,0:T(8,128)(2,1)S(1)} %get-tuple-element.15.refs_0_, bf16[3072,128]{1,0:T(8,128)(2,1)S(1)} %get-tuple-element.16.refs_1_.refs_2_, bf16[3072,128]{1,0:T(8,128)(2,1)S(1)} %collective-permute-done.refs_2_.refs_3_, bf16[3072,128]{1,0:T(8,128)(2,1)S(1)} %collective-permute-done.1.refs_3_.refs_4_), custom_call_target="tpu_custom_call" | custom-call | flops 1000000000 | bytes 1572864 | tf_op jit(solution)/shard_map/attend/pallas_call | solution.py:258
  87.0 2.3 %collective-permute-done.4.refs_1_ = bf16[1584,128]{1,0:T(8,128)(2,1)S(1)} collective-permute-done((bf16[1584,128]{1,0:T(8,128)(2,1)S(1)}, bf16[1584,128]{1,0:T(8,128)(2,1)S(1)}, u32[]{:S(2)}, u32[]{:S(2)}) %collective-permute-start.4) | collective-permute-done | bytes 405536 | tf_op jit(solution)/shard_map/ppermute | solution.py:31
  89.3 4.4 %collective-permute-done.5.refs_2_ = bf16[1584,128]{1,0:T(8,128)(2,1)S(1)} collective-permute-done((bf16[1584,128]{1,0:T(8,128)(2,1)S(1)}, bf16[1584,128]{1,0:T(8,128)(2,1)S(1)}, u32[]{:S(2)}, u32[]{:S(2)}) %collective-permute-start.5) | collective-permute-done | bytes 405536 | tf_op jit(solution)/shard_map/ppermute | solution.py:31
  93.7 1.2 %finish.1 = bf16[1,8,32,1536]{3,2,1,0:T(8,128)(2,1)} custom-call(s32[8,128]{1,0:T(8,128)S(1)} %get-tuple-element.14.ok_ref, f32[776,256]{1,0:T(8,128)S(1)} %attend.4.refs_0_, bf16[1584,128]{1,0:T(8,128)(2,1)S(1)} %collective-permute-done.4.refs_1_, bf16[1584,128]{1,0:T(8,128)(2,1)S(1)} %collective-permute-done.5.refs_2_, ...), custom_call_target="tpu_custom_call" | custom-call | flops 100000000 | bytes 3145728 | tf_op jit(solution)/shard_map/finish/pallas_call | solution.py:343
  (7 shorter events, 0.2 us)
Async XLA Ops:
  2.2 52.4 %collective-permute-start = (bf16[3072,128]{1,0:T(8,128)(2,1)S(1)}, bf16[3072,128]{1,0:T(8,128)(2,1)S(1)}, u32[]{:S(2)}, u32[]{:S(2)}) collective-permute-start(bf16[3072,128]{1,0:T(8,128)(2,1)S(1)} %get-tuple-element.16.refs_1_.refs_2_), channel_id=1, source_target_pairs={{0,8},{8,16},{16,24},{24,32},{32,40},{40,48},{48,56},{56,64},{64,7... | collective-permute-start | bytes 2359304 | tf_op jit(solution)/shard_map/ppermute | solution.py:31
  6.9 43.2 %collective-permute-start.6 = (bf16[1584,128]{1,0:T(8,128)(2,1)S(1)}, bf16[1584,128]{1,0:T(8,128)(2,1)S(1)}, u32[]{:S(2)}, u32[]{:S(2)}) collective-permute-start(bf16[1584,128]{1,0:T(8,128)(2,1)S(1)} %get-tuple-element.19.refs_1_), channel_id=1, source_target_pairs={{8,0},{16,8},{24,16},{32,24},{40,32},{48,40},{56,48},{64,56},{72,6... | collective-permute-start | bytes 1216520 | tf_op jit(solution)/shard_map/ppermute | solution.py:31
  44.7 11.4 %collective-permute-start.7 = (bf16[3072,128]{1,0:T(8,128)(2,1)S(1)}, bf16[3072,128]{1,0:T(8,128)(2,1)S(1)}, u32[]{:S(2)}, u32[]{:S(2)}) collective-permute-start(bf16[3072,128]{1,0:T(8,128)(2,1)S(1)} %get-tuple-element.20.refs_3_.refs_2_), channel_id=1, source_target_pairs={{0,2},{2,4},{4,6},{1,3},{3,5},{5,7},{8,10},{10,12},{12,14},{9,11},... | collective-permute-start | bytes 2359304 | tf_op jit(solution)/shard_map/ppermute | solution.py:31
  46.1 14.1 %collective-permute-start.8 = (bf16[3072,128]{1,0:T(8,128)(2,1)S(1)}, bf16[3072,128]{1,0:T(8,128)(2,1)S(1)}, u32[]{:S(2)}, u32[]{:S(2)}) collective-permute-start(bf16[3072,128]{1,0:T(8,128)(2,1)S(1)} %get-tuple-element.20.refs_3_.refs_2_), channel_id=1, source_target_pairs={{2,0},{4,2},{6,4},{3,1},{5,3},{7,5},{10,8},{12,10},{14,12},{11,9},... | collective-permute-start | bytes 2359304 | tf_op jit(solution)/shard_map/ppermute | solution.py:31
  50.1 10.1 %collective-permute-start.9 = (bf16[1584,128]{1,0:T(8,128)(2,1)S(1)}, bf16[1584,128]{1,0:T(8,128)(2,1)S(1)}, u32[]{:S(2)}, u32[]{:S(2)}) collective-permute-start(bf16[1584,128]{1,0:T(8,128)(2,1)S(1)} %collective-permute-done.6.refs_0_), channel_id=1, source_target_pairs={{8,0},{16,8},{24,16},{32,24},{40,32},{48,40},{56,48},{64,56},{72,6... | collective-permute-start | bytes 1216520 | tf_op jit(solution)/shard_map/ppermute | solution.py:31
  54.6 22.3 %collective-permute-start.1 = (bf16[3072,128]{1,0:T(8,128)(2,1)S(1)}, bf16[3072,128]{1,0:T(8,128)(2,1)S(1)}, u32[]{:S(2)}, u32[]{:S(2)}) collective-permute-start(bf16[3072,128]{1,0:T(8,128)(2,1)S(1)} %collective-permute-done.refs_2_.refs_3_), channel_id=1, source_target_pairs={{8,16},{16,24},{24,32},{32,40},{40,48},{48,56},{56,64},{64,72},{72... | collective-permute-start | bytes 2359304 | tf_op jit(solution)/shard_map/ppermute | solution.py:31
  62.1 9.8 %collective-permute-start.10 = (bf16[1584,128]{1,0:T(8,128)(2,1)S(1)}, bf16[1584,128]{1,0:T(8,128)(2,1)S(1)}, u32[]{:S(2)}, u32[]{:S(2)}) collective-permute-start(bf16[1584,128]{1,0:T(8,128)(2,1)S(1)} %attend.7), channel_id=1, source_target_pairs={{0,8},{8,16},{16,24},{24,32},{32,40},{40,48},{48,56},{56,64},{64,7... | collective-permute-start | bytes 1216520 | tf_op jit(solution)/shard_map/ppermute | solution.py:31
  64.0 12.3 %collective-permute-start.2 = (bf16[1584,128]{1,0:T(8,128)(2,1)S(1)}, bf16[1584,128]{1,0:T(8,128)(2,1)S(1)}, u32[]{:S(2)}, u32[]{:S(2)}) collective-permute-start(bf16[1584,128]{1,0:T(8,128)(2,1)S(1)} %get-tuple-element.15.refs_0_), channel_id=1, source_target_pairs={{0,2},{2,4},{4,6},{1,3},{3,5},{5,7},{8,10},{10,12},{12,14},{9,11},... | collective-permute-start | bytes 1216520 | tf_op jit(solution)/shard_map/ppermute | solution.py:31
  65.7 11.2 %collective-permute-start.3 = (bf16[1584,128]{1,0:T(8,128)(2,1)S(1)}, bf16[1584,128]{1,0:T(8,128)(2,1)S(1)}, u32[]{:S(2)}, u32[]{:S(2)}) collective-permute-start(bf16[1584,128]{1,0:T(8,128)(2,1)S(1)} %get-tuple-element.15.refs_0_), channel_id=1, source_target_pairs={{2,0},{4,2},{6,4},{3,1},{5,3},{7,5},{10,8},{12,10},{14,12},{11,9},... | collective-permute-start | bytes 1216520 | tf_op jit(solution)/shard_map/ppermute | solution.py:31
  72.1 14.9 %collective-permute-start.11 = (bf16[1584,128]{1,0:T(8,128)(2,1)S(1)}, bf16[1584,128]{1,0:T(8,128)(2,1)S(1)}, u32[]{:S(2)}, u32[]{:S(2)}) collective-permute-start(bf16[1584,128]{1,0:T(8,128)(2,1)S(1)} %merge.1), channel_id=1, source_target_pairs={{0,8},{8,16},{16,24},{24,32},{32,40},{40,48},{48,56},{56,64},{64,7... | collective-permute-start | bytes 1216520 | tf_op jit(solution)/shard_map/ppermute | solution.py:31
  80.2 9.1 %collective-permute-start.4 = (bf16[1584,128]{1,0:T(8,128)(2,1)S(1)}, bf16[1584,128]{1,0:T(8,128)(2,1)S(1)}, u32[]{:S(2)}, u32[]{:S(2)}) collective-permute-start(bf16[1584,128]{1,0:T(8,128)(2,1)S(1)} %get-tuple-element.17), channel_id=1, source_target_pairs={{0,2},{2,4},{4,6},{1,3},{3,5},{5,7},{8,10},{10,12},{12,14},{9,11},... | collective-permute-start | bytes 1216520 | tf_op jit(solution)/shard_map/ppermute | solution.py:31
  83.9 9.8 %collective-permute-start.5 = (bf16[1584,128]{1,0:T(8,128)(2,1)S(1)}, bf16[1584,128]{1,0:T(8,128)(2,1)S(1)}, u32[]{:S(2)}, u32[]{:S(2)}) collective-permute-start(bf16[1584,128]{1,0:T(8,128)(2,1)S(1)} %get-tuple-element.18), channel_id=1, source_target_pairs={{2,0},{4,2},{6,4},{3,1},{5,3},{7,5},{10,8},{12,10},{14,12},{11,9},... | collective-permute-start | bytes 1216520 | tf_op jit(solution)/shard_map/ppermute | solution.py:31

commit v2 on v1

--- a/solution.py
+++ b/solution.py
@@ -59,23 +59,20 @@
     table.start()
     rows, cols = q_ref.shape[1], q_ref.shape[2]
     copies = {}
-    for half in range(2):
-        qc_ref, kv_ref = packed[2 * half : 2 * half + 2]
-        for j in range(heads):
-            head = half * heads + j
-            lanes = pl.ds(head * HDIM, HDIM)
-            at = pl.ds(j * tokens, tokens)
-            slot = pl.ds(head * tokens, tokens)
-            for n, (src, dst) in enumerate(
-                ((v_ref, vbuf.at[slot]), (k_ref, kv_ref.at[at]), (q_ref, qc_ref.at[at]))
-            ):
-                copy = pltpu.make_async_copy(
-                    src.at[0, :, :, lanes],
-                    dst.reshape(rows, cols, HDIM),
-                    sems.at[3 * head + n],
-                )
-                copy.start()
-                copies[half, j, n] = copy
+    for n, src in enumerate((v_ref, k_ref, q_ref)):
+        for head in range(2 * heads):
+            half, j = divmod(head, heads)
+            if n == 0:
+                dst = vbuf.at[pl.ds(head * tokens, tokens)]
+            else:
+                dst = packed[2 * half + n % 2].at[pl.ds(j * tokens, tokens)]
+            copy = pltpu.make_async_copy(
+                src.at[0, :, :, pl.ds(head * HDIM, HDIM)],
+                dst.reshape(rows, cols, HDIM),
+                sems.at[3 * head + n],
+            )
+            copy.start()
+            copies[n, head] = copy
     here, frame = lax.axis_index("space"), lax.axis_index("tm")
     tests = here > 0, here < lax.axis_size("space") - 1, frame > 0, frame > 1
     flags = [jnp.where(test, 1, 0) for test in tests]
@@ -87,21 +84,18 @@
     table.wait()
     mask = masks(cols // TILE, flags, wbuf[...].astype(jnp.float32))
     for half in range(2):
-        qc_ref, kv_ref = packed[2 * half : 2 * half + 2]
-        qc_ref[heads * tokens :, :] = mask
-        for j in range(heads):
-            copies[half, j, 0].wait()
-            slot = (half * heads + j) * tokens
-            vt = vbuf[slot : slot + tokens, :].T
-            base = (heads + j) * tokens
-            for s in range(tokens // HDIM):
-                kv_ref[base + s * HDIM : base + (s + 1) * HDIM, :] = vt[
-                    :, s * HDIM : (s + 1) * HDIM
-                ]
-    for half in range(2):
-        for j in range(heads):
-            copies[half, j, 1].wait()
-            copies[half, j, 2].wait()
+        packed[2 * half][heads * tokens :, :] = mask
+    for head in range(2 * heads):
+        copies[0, head].wait()
+    for head in range(2 * heads):
+        half, j = divmod(head, heads)
+        vt = vbuf[head * tokens : (head + 1) * tokens, :].T
+        for s in range(tokens // HDIM):
+            at = (heads + j) * tokens + s * HDIM
+            packed[2 * half + 1][at : at + HDIM, :] = vt[:, s * HDIM : (s + 1) * HDIM]
+    for head in range(2 * heads):
+        copies[1, head].wait()
+        copies[2, head].wait()
 
 
 def pack(heads, queries, keys, values, window):
@@ -161,10 +155,26 @@
     return jnp.concatenate(parts, axis=1)
 
 
-def attend_kernel(heads, tokens, cols, sets, packed, *refs):
+def attend_kernel(heads, tokens, cols, sets, packed, cases, *refs):
     q_refs, refs = refs[: len(sets)], refs[len(sets) :]
     blocks = len(sets[0])
-    kvs, refs = refs[:blocks], refs[blocks:]
+    kvs, out_refs = refs[:blocks], refs[blocks:]
+    run = functools.partial(attend_case, heads, tokens, cols, sets, packed, q_refs, kvs, out_refs)
+    everything = tuple(range(len(sets))), tuple(range(blocks))
+    rest = None
+    for where, chosen, used in (*cases, ((), *everything)):
+        hit = rest
+        for axis, index in where:
+            same = lax.axis_index(axis) == index % lax.axis_size(axis)
+            hit = same if hit is None else hit & same
+        if hit is None:
+            run(chosen, used)
+            return
+        pl.when(hit)(functools.partial(run, chosen, used))
+        rest = jnp.logical_not(hit) if rest is None else rest & jnp.logical_not(hit)
+
+
+def attend_case(heads, tokens, cols, sets, packed, q_refs, kvs, out_refs, chosen, used):
     tcols = cols // TILE
     repeat = tokens // cols
 
@@ -173,27 +183,27 @@
     tile = jnp.where(lane == lax.div(row, TILE), 1.0, 0.0).astype(jnp.bfloat16)
     tile = jnp.concatenate([tile] * repeat, axis=0)
     bias = {}
-    for which, places in enumerate(sets):
+    for which in chosen:
         rows = q_refs[which][heads * tokens :, :].astype(jnp.float32)
-        for n, place in enumerate(places):
+        for n in used:
+            at = sets[which][n] * tcols
             part = [
-                jnp.broadcast_to(rows[place * tcols + c : place * tcols + c + 1, :], (TILE, HDIM))
-                for c in range(tcols)
+                jnp.broadcast_to(rows[at + c : at + c + 1, :], (TILE, HDIM)) for c in range(tcols)
             ]
             part = jnp.concatenate(part, axis=0).astype(jnp.bfloat16)
             bias[which, n] = jnp.concatenate([part] * repeat, axis=0)
 
-    streams = [(which, j) for which in range(len(sets)) for j in range(heads)]
+    streams = [(which, j) for which in chosen for j in range(heads)]
     group = 3 if len(streams) % 3 == 0 else 1
     units = [
         (n, stream)
         for base in range(0, len(streams), group)
-        for n in range(blocks)
+        for n in used
         for stream in streams[base : base + group]
     ]
     tops, totals, outs, ready = {}, {}, {}, {}
     sub = lax.broadcasted_iota(jnp.int32, (STATS, tokens), 0)
-    lses = [jnp.full((STATS, tokens), NEVER, jnp.float32) for _ in sets]
+    lses = {which: jnp.full((STATS, tokens), NEVER, jnp.float32) for which in chosen}
     for i in range(len(units) + LAG):
         if i < len(units):
             n, key = units[i]
@@ -223,22 +233,22 @@
                 preferred_element_type=jnp.float32,
             )
             outs[key] = out if fade is None else outs[key] * fade + out
-            if n == blocks - 1:
+            if n == used[-1]:
                 total = totals[key]
                 out = outs.pop(key) * (1.0 / jnp.maximum(total, 1e-30))
                 lse = tops[key] + jnp.log2(total)
                 lses[which] = jnp.where((sub == j) & (total > 0), lse, lses[which])
                 if packed[which]:
                     write_partial(
-                        refs[which], heads, tokens, [(j, out.astype(jnp.bfloat16))], None
+                        out_refs[which], heads, tokens, [(j, out.astype(jnp.bfloat16))], None
                     )
                 else:
-                    refs[which][j * HDIM : (j + 1) * HDIM, :] = out
-    for which, lse in enumerate(lses):
+                    out_refs[which][j * HDIM : (j + 1) * HDIM, :] = out
+    for which, lse in lses.items():
         if packed[which]:
-            write_partial(refs[which], heads, tokens, [], lse)
+            write_partial(out_refs[which], heads, tokens, [], lse)
         else:
-            refs[which][heads * HDIM :, :] = lse
+            out_refs[which][heads * HDIM :, :] = lse
 
 
 def partial_shape(heads, tokens):
@@ -246,7 +256,7 @@
     return jax.ShapeDtypeStruct((heads * tokens + stats, HDIM), jnp.bfloat16)
 
 
-def attend(sets, packed, heads, shape, qs, kvs):
+def attend(sets, packed, cases, heads, shape, qs, kvs):
     rows, cols, _ = shape
     tokens = rows * cols
     out_shape = [
@@ -256,7 +266,7 @@
         for p in packed
     ]
     return pl.pallas_call(
-        functools.partial(attend_kernel, heads, tokens, cols, sets, packed),
+        functools.partial(attend_kernel, heads, tokens, cols, sets, packed, cases),
         out_shape=out_shape,
         in_specs=[WHOLE] * (len(qs) + len(kvs)),
         out_specs=[WHOLE] * len(packed),
@@ -374,10 +384,19 @@
     along = (kva, a1, a2)
     frames = [tuple(3 * back + dy for back in range(3)) for dy in range(3)]
     both, mine = (True, True), (False,)
-    km, kp = go((frames[2], frames[0]), both, qs=(qm, qp), kvs=along)
+    first, second, edge = ("tm", 0), ("tm", 1), ("space", 0)
+    pair_cases = (
+        ((first, edge), (1,), (0,)),
+        ((first,), (0, 1), (0,)),
+        ((second, edge), (1,), (0, 1)),
+        ((second,), (0, 1), (0, 1)),
+    )
+    frame_cases = (((first,), (0,), (0,)), ((second,), (0,), (0, 1)))
+    row_cases = (((edge,), (0,), (1, 2)), ((("space", -1),), (0,), (0, 1)))
+    km, kp = go((frames[2], frames[0]), both, pair_cases, qs=(qm, qp), kvs=along)
     pp = shift(km, "space", -1)
     pm = shift(kp, "space", 1)
-    (ka,) = go((frames[1],), mine, qs=(qa,), kvs=along)
+    (ka,) = go((frames[1],), mine, frame_cases, qs=(qa,), kvs=along)
 
     q1 = shift(qb, "tm", -1)
     q2 = shift(q1, "tm", -1, ahead=1)
@@ -386,9 +405,10 @@
     across = (lo, kvb, hi)
     offsets = [tuple(3 * back + dy for dy in range(3)) for back in range(3)]
 
-    (k2,) = go((offsets[2],), (True,), qs=(q2,), kvs=across)
+    (k2,) = go((offsets[2],), (True,), row_cases, qs=(q2,), kvs=across)
     p2 = shift(k2, "tm", 1, ahead=1)
-    k1, k0 = go((offsets[1], offsets[0]), (False, False), qs=(q1, qb), kvs=across)
+    (k1,) = go((offsets[1],), mine, row_cases, qs=(q1,), kvs=across)
+    (k0,) = go((offsets[0],), mine, row_cases, qs=(qb,), kvs=across)
     m1 = merge(half, shape, ok, k1, (p2,), (FRAME_1,))
     p1 = shift(m1, "tm", 1)
 

time: 95.4 us -> 93.6 us (0.981)
  Pallas kernels: 13.8 us -> 10.1 us
  starting transfers between devices: 65.3 us -> 66.7 us
    pallas_call x4 -> x5, Pallas kernels: 10.3 us -> 6.71 us  [attend(): pl.pallas_call(functools.partial(attend_kernel, heads, tokens, cols, sets...]
    ppermute x12, starting transfers between devices: 65.3 us -> 66.7 us  [shift(): return lax.ppermute(block, axis, route)]
  transfers between devices with their start and end apart: 12 -> 12, of which waited for: 6 -> 6; matrix products, arithmetic and copies ran while one was open for 0% -> 0% of each run, Pallas kernels for 11% -> 7%
where the time goes in v2:
time: 93.6 us; the launch traced here: 93.1 us
  starting transfers between devices  66.7 us (71%)
  waiting for transfers between devices  16 us (17%)
  Pallas kernels  10.1 us (11%)
    ppermute x12, starting transfers between devices, shift(): return lax.ppermute(block, axis, route)  66.7 us
    ppermute x12, waiting for transfers between devices, shift(): return lax.ppermute(block, axis, route)  16 us
    pallas_call x5, Pallas kernels, attend(): pl.pallas_call(functools.partial(attend_kernel, heads, tokens, cols, sets...  6.71 us
    pallas_call x1, Pallas kernels, pack(): pl.pallas_call(functools.partial(pack_kernel, heads, tokens), out_shape=s...  2.04 us
  transfers between devices with their start and end apart: 12, of which 6 were waited for; matrix products, arithmetic and copies ran while one was open for 0% of the time, Pallas kernels for 7%

profile of v2, /device:TPU:160, one launch (start us, length us, event | category | flops | bytes accessed | tf_op | source)
XLA Modules:
  0.0 93.1 jit_solution(7543253086155542731)
XLA Ops:
  0.0 2.0 %pack.1 = (bf16[1584,128]{1,0:T(8,128)(2,1)S(1)}, bf16[3072,128]{1,0:T(8,128)(2,1)S(1)}, bf16[1584,128]{1,0:T(8,128)(2,1)S(1)}, bf16[3072,128]{1,0:T(8,128)(2,1)S(1)}, s32[8,128]{1,0:T(8,128)S(1)}) custom-call(bf16[1,8,32,1536]{3,2,1,0:T(8,128)(2,1)} %q_ref.1, bf16[1,8,32,1536]{3,2,1,0:T(8,128)(2,1)} %k_ref.1, bf16[1,8,32,1536]{3,2,1,0:T(8,128)(2,1)} %v_ref.1, ...), custom_call_target="tpu_custom_call" | custom-call | flops 1000000000 | bytes 2359296 | tf_op jit(solution)/shard_map/pack/pallas_call | solution.py:107
  2.0 4.7 %collective-permute-start = (bf16[3072,128]{1,0:T(8,128)(2,1)S(1)}, bf16[3072,128]{1,0:T(8,128)(2,1)S(1)}, u32[]{:S(2)}, u32[]{:S(2)}) collective-permute-start(bf16[3072,128]{1,0:T(8,128)(2,1)S(1)} %get-tuple-element.14.refs_1_.refs_2_), channel_id=1, source_target_pairs={{0,8},{8,16},{16,24},{24,32},{32,40},{40,48},{48,56},{56,64},{64,7... | collective-permute-start | bytes 2359304 | tf_op jit(solution)/shard_map/ppermute | solution.py:31
  6.8 37.8 %collective-permute-start.8 = (bf16[1584,128]{1,0:T(8,128)(2,1)S(1)}, bf16[1584,128]{1,0:T(8,128)(2,1)S(1)}, u32[]{:S(2)}, u32[]{:S(2)}) collective-permute-start(bf16[1584,128]{1,0:T(8,128)(2,1)S(1)} %get-tuple-element.17.refs_0_), channel_id=1, source_target_pairs={{8,0},{16,8},{24,16},{32,24},{40,32},{48,40},{56,48},{64,56},{72,6... | collective-permute-start | bytes 1216520 | tf_op jit(solution)/shard_map/ppermute | solution.py:31
  44.6 1.4 %collective-permute-start.6 = (bf16[3072,128]{1,0:T(8,128)(2,1)S(1)}, bf16[3072,128]{1,0:T(8,128)(2,1)S(1)}, u32[]{:S(2)}, u32[]{:S(2)}) collective-permute-start(bf16[3072,128]{1,0:T(8,128)(2,1)S(1)} %get-tuple-element.18.refs_2_), channel_id=1, source_target_pairs={{0,2},{2,4},{4,6},{1,3},{3,5},{5,7},{8,10},{10,12},{12,14},{9,11},... | collective-permute-start | bytes 2359304 | tf_op jit(solution)/shard_map/ppermute | solution.py:31
  46.0 1.3 %collective-permute-start.7 = (bf16[3072,128]{1,0:T(8,128)(2,1)S(1)}, bf16[3072,128]{1,0:T(8,128)(2,1)S(1)}, u32[]{:S(2)}, u32[]{:S(2)}) collective-permute-start(bf16[3072,128]{1,0:T(8,128)(2,1)S(1)} %get-tuple-element.18.refs_2_), channel_id=1, source_target_pairs={{2,0},{4,2},{6,4},{3,1},{5,3},{7,5},{10,8},{12,10},{14,12},{11,9},... | collective-permute-start | bytes 2359304 | tf_op jit(solution)/shard_map/ppermute | solution.py:31
  47.3 2.7 %collective-permute-done.8.refs_0_ = bf16[1584,128]{1,0:T(8,128)(2,1)S(1)} collective-permute-done((bf16[1584,128]{1,0:T(8,128)(2,1)S(1)}, bf16[1584,128]{1,0:T(8,128)(2,1)S(1)}, u32[]{:S(2)}, u32[]{:S(2)}) %collective-permute-start.8) | collective-permute-done | bytes 405536 | tf_op jit(solution)/shard_map/ppermute | solution.py:31
  50.0 4.4 %collective-permute-start.9 = (bf16[1584,128]{1,0:T(8,128)(2,1)S(1)}, bf16[1584,128]{1,0:T(8,128)(2,1)S(1)}, u32[]{:S(2)}, u32[]{:S(2)}) collective-permute-start(bf16[1584,128]{1,0:T(8,128)(2,1)S(1)} %collective-permute-done.8.refs_0_), channel_id=1, source_target_pairs={{8,0},{16,8},{24,16},{32,24},{40,32},{48,40},{56,48},{64,56},{72,6... | collective-permute-start | bytes 1216520 | tf_op jit(solution)/shard_map/ppermute | solution.py:31
  55.0 1.3 %collective-permute-start.1 = (bf16[3072,128]{1,0:T(8,128)(2,1)S(1)}, bf16[3072,128]{1,0:T(8,128)(2,1)S(1)}, u32[]{:S(2)}, u32[]{:S(2)}) collective-permute-start(bf16[3072,128]{1,0:T(8,128)(2,1)S(1)} %collective-permute-done.refs_2_.refs_3_), channel_id=1, source_target_pairs={{8,16},{16,24},{24,32},{32,40},{40,48},{48,56},{56,64},{64,72},{72... | collective-permute-start | bytes 2359304 | tf_op jit(solution)/shard_map/ppermute | solution.py:31
  56.4 3.7 %collective-permute-done.7.refs_3_ = bf16[3072,128]{1,0:T(8,128)(2,1)S(1)} collective-permute-done((bf16[3072,128]{1,0:T(8,128)(2,1)S(1)}, bf16[3072,128]{1,0:T(8,128)(2,1)S(1)}, u32[]{:S(2)}, u32[]{:S(2)}) %collective-permute-start.7) | collective-permute-done | bytes 786464 | tf_op jit(solution)/shard_map/ppermute | solution.py:31
  60.1 1.3 %attend.9 = bf16[1584,128]{1,0:T(8,128)(2,1)S(1)} custom-call(bf16[1584,128]{1,0:T(8,128)(2,1)S(1)} %collective-permute-done.9.refs_0_, bf16[3072,128]{1,0:T(8,128)(2,1)S(1)} %collective-permute-done.6.refs_1_, bf16[3072,128]{1,0:T(8,128)(2,1)S(1)} %get-tuple-element.18.refs_2_, bf16[3072,128]{1,0:T(8,128)(2,1)S(1)} %collective-permute-done.7.refs_3_), custom_call_target="tpu_custom_call" | custom-call | flops 1000000000 | bytes 1572864 | tf_op jit(solution)/shard_map/attend/pallas_call | solution.py:268
  61.4 2.0 %collective-permute-start.10 = (bf16[1584,128]{1,0:T(8,128)(2,1)S(1)}, bf16[1584,128]{1,0:T(8,128)(2,1)S(1)}, u32[]{:S(2)}, u32[]{:S(2)}) collective-permute-start(bf16[1584,128]{1,0:T(8,128)(2,1)S(1)} %attend.9), channel_id=1, source_target_pairs={{0,8},{8,16},{16,24},{24,32},{32,40},{40,48},{48,56},{56,64},{64,7... | collective-permute-start | bytes 1216520 | tf_op jit(solution)/shard_map/ppermute | solution.py:31
  63.4 2.2 %collective-permute-start.2 = (bf16[1584,128]{1,0:T(8,128)(2,1)S(1)}, bf16[1584,128]{1,0:T(8,128)(2,1)S(1)}, u32[]{:S(2)}, u32[]{:S(2)}) collective-permute-start(bf16[1584,128]{1,0:T(8,128)(2,1)S(1)} %get-tuple-element.13.refs_0_), channel_id=1, source_target_pairs={{0,2},{2,4},{4,6},{1,3},{3,5},{5,7},{8,10},{10,12},{12,14},{9,11},... | collective-permute-start | bytes 1216520 | tf_op jit(solution)/shard_map/ppermute | solution.py:31
  65.5 1.3 %collective-permute-start.3 = (bf16[1584,128]{1,0:T(8,128)(2,1)S(1)}, bf16[1584,128]{1,0:T(8,128)(2,1)S(1)}, u32[]{:S(2)}, u32[]{:S(2)}) collective-permute-start(bf16[1584,128]{1,0:T(8,128)(2,1)S(1)} %get-tuple-element.13.refs_0_), channel_id=1, source_target_pairs={{2,0},{4,2},{6,4},{3,1},{5,3},{7,5},{10,8},{12,10},{14,12},{11,9},... | collective-permute-start | bytes 1216520 | tf_op jit(solution)/shard_map/ppermute | solution.py:31
  66.8 1.3 %attend.8.local = f32[776,256]{1,0:T(8,128)S(1)} custom-call(bf16[1584,128]{1,0:T(8,128)(2,1)S(1)} %collective-permute-done.8.refs_0_, bf16[3072,128]{1,0:T(8,128)(2,1)S(1)} %collective-permute-done.6.refs_1_, bf16[3072,128]{1,0:T(8,128)(2,1)S(1)} %get-tuple-element.18.refs_2_, bf16[3072,128]{1,0:T(8,128)(2,1)S(1)} %collective-permute-done.7.refs_3_), custom_call_target="tpu_custom_call" | custom-call | flops 1000000000 | bytes 1572864 | tf_op jit(solution)/shard_map/attend/pallas_call | solution.py:268
  68.2 3.1 %collective-permute-done.10.refs_0_ = bf16[1584,128]{1,0:T(8,128)(2,1)S(1)} collective-permute-done((bf16[1584,128]{1,0:T(8,128)(2,1)S(1)}, bf16[1584,128]{1,0:T(8,128)(2,1)S(1)}, u32[]{:S(2)}, u32[]{:S(2)}) %collective-permute-start.10) | collective-permute-done | bytes 405536 | tf_op jit(solution)/shard_map/ppermute | solution.py:31
  71.4 4.8 %collective-permute-start.11 = (bf16[1584,128]{1,0:T(8,128)(2,1)S(1)}, bf16[1584,128]{1,0:T(8,128)(2,1)S(1)}, u32[]{:S(2)}, u32[]{:S(2)}) collective-permute-start(bf16[1584,128]{1,0:T(8,128)(2,1)S(1)} %merge.1), channel_id=1, source_target_pairs={{0,8},{8,16},{16,24},{24,32},{32,40},{40,48},{48,56},{56,64},{64,7... | collective-permute-start | bytes 1216520 | tf_op jit(solution)/shard_map/ppermute | solution.py:31
  76.3 1.5 %attend.6 = (bf16[1584,128]{1,0:T(8,128)(2,1)S(1)}, bf16[1584,128]{1,0:T(8,128)(2,1)S(1)}) custom-call(bf16[1584,128]{1,0:T(8,128)(2,1)S(1)} %collective-permute-done.2.refs_0_, bf16[1584,128]{1,0:T(8,128)(2,1)S(1)} %collective-permute-done.3.refs_1_, bf16[3072,128]{1,0:T(8,128)(2,1)S(1)} %get-tuple-element.14.refs_1_.refs_2_, ...), custom_call_target="tpu_custom_call" | custom-call | flops 1000000000 | bytes 1572864 | tf_op jit(solution)/shard_map/attend/pallas_call | solution.py:268
  77.8 4.1 %collective-permute-start.4 = (bf16[1584,128]{1,0:T(8,128)(2,1)S(1)}, bf16[1584,128]{1,0:T(8,128)(2,1)S(1)}, u32[]{:S(2)}, u32[]{:S(2)}) collective-permute-start(bf16[1584,128]{1,0:T(8,128)(2,1)S(1)} %get-tuple-element.15), channel_id=1, source_target_pairs={{0,2},{2,4},{4,6},{1,3},{3,5},{5,7},{8,10},{10,12},{12,14},{9,11},... | collective-permute-start | bytes 1216520 | tf_op jit(solution)/shard_map/ppermute | solution.py:31
  81.9 1.3 %collective-permute-start.5 = (bf16[1584,128]{1,0:T(8,128)(2,1)S(1)}, bf16[1584,128]{1,0:T(8,128)(2,1)S(1)}, u32[]{:S(2)}, u32[]{:S(2)}) collective-permute-start(bf16[1584,128]{1,0:T(8,128)(2,1)S(1)} %get-tuple-element.16), channel_id=1, source_target_pairs={{2,0},{4,2},{6,4},{3,1},{5,3},{7,5},{10,8},{12,10},{14,12},{11,9},... | collective-permute-start | bytes 1216520 | tf_op jit(solution)/shard_map/ppermute | solution.py:31
  83.2 1.3 %attend.7.refs_3_ = f32[776,256]{1,0:T(8,128)S(1)} custom-call(bf16[1584,128]{1,0:T(8,128)(2,1)S(1)} %get-tuple-element.17.refs_0_, bf16[3072,128]{1,0:T(8,128)(2,1)S(1)} %collective-permute-done.6.refs_1_, bf16[3072,128]{1,0:T(8,128)(2,1)S(1)} %get-tuple-element.18.refs_2_, bf16[3072,128]{1,0:T(8,128)(2,1)S(1)} %collective-permute-done.7.refs_3_), custom_call_target="tpu_custom_call" | custom-call | flops 1000000000 | bytes 1572864 | tf_op jit(solution)/shard_map/attend/pallas_call | solution.py:268
  84.6 1.3 %attend.5.refs_0_ = f32[776,256]{1,0:T(8,128)S(1)} custom-call(bf16[1584,128]{1,0:T(8,128)(2,1)S(1)} %get-tuple-element.13.refs_0_, bf16[3072,128]{1,0:T(8,128)(2,1)S(1)} %get-tuple-element.14.refs_1_.refs_2_, bf16[3072,128]{1,0:T(8,128)(2,1)S(1)} %collective-permute-done.refs_2_.refs_3_, bf16[3072,128]{1,0:T(8,128)(2,1)S(1)} %collective-permute-done.1.refs_3_.refs_4_), custom_call_target="tpu_custom_call" | custom-call | flops 1000000000 | bytes 1572864 | tf_op jit(solution)/shard_map/attend/pallas_call | solution.py:268
  85.9 1.4 %collective-permute-done.4.refs_1_ = bf16[1584,128]{1,0:T(8,128)(2,1)S(1)} collective-permute-done((bf16[1584,128]{1,0:T(8,128)(2,1)S(1)}, bf16[1584,128]{1,0:T(8,128)(2,1)S(1)}, u32[]{:S(2)}, u32[]{:S(2)}) %collective-permute-start.4) | collective-permute-done | bytes 405536 | tf_op jit(solution)/shard_map/ppermute | solution.py:31
  87.3 4.4 %collective-permute-done.5.refs_2_ = bf16[1584,128]{1,0:T(8,128)(2,1)S(1)} collective-permute-done((bf16[1584,128]{1,0:T(8,128)(2,1)S(1)}, bf16[1584,128]{1,0:T(8,128)(2,1)S(1)}, u32[]{:S(2)}, u32[]{:S(2)}) %collective-permute-start.5) | collective-permute-done | bytes 405536 | tf_op jit(solution)/shard_map/ppermute | solution.py:31
  91.8 1.2 %finish.1 = bf16[1,8,32,1536]{3,2,1,0:T(8,128)(2,1)} custom-call(s32[8,128]{1,0:T(8,128)S(1)} %get-tuple-element.12.ok_ref, f32[776,256]{1,0:T(8,128)S(1)} %attend.5.refs_0_, bf16[1584,128]{1,0:T(8,128)(2,1)S(1)} %collective-permute-done.4.refs_1_, bf16[1584,128]{1,0:T(8,128)(2,1)S(1)} %collective-permute-done.5.refs_2_, f32[776,256]{1,0:T(8,128)S(1)} %attend.7.refs_3_, ...), custom_call_target="tpu_custom_call" | custom-call | flops 100000000 | bytes 3145728 | tf_op jit(solution)/shard_map/finish/pallas_call | solution.py:353
  (8 shorter events, 0.8 us)
Async XLA Ops:
  2.0 53.0 %collective-permute-start = (bf16[3072,128]{1,0:T(8,128)(2,1)S(1)}, bf16[3072,128]{1,0:T(8,128)(2,1)S(1)}, u32[]{:S(2)}, u32[]{:S(2)}) collective-permute-start(bf16[3072,128]{1,0:T(8,128)(2,1)S(1)} %get-tuple-element.14.refs_1_.refs_2_), channel_id=1, source_target_pairs={{0,8},{8,16},{16,24},{24,32},{32,40},{40,48},{48,56},{56,64},{64,7... | collective-permute-start | bytes 2359304 | tf_op jit(solution)/shard_map/ppermute | solution.py:31
  6.8 43.2 %collective-permute-start.8 = (bf16[1584,128]{1,0:T(8,128)(2,1)S(1)}, bf16[1584,128]{1,0:T(8,128)(2,1)S(1)}, u32[]{:S(2)}, u32[]{:S(2)}) collective-permute-start(bf16[1584,128]{1,0:T(8,128)(2,1)S(1)} %get-tuple-element.17.refs_0_), channel_id=1, source_target_pairs={{8,0},{16,8},{24,16},{32,24},{40,32},{48,40},{56,48},{64,56},{72,6... | collective-permute-start | bytes 1216520 | tf_op jit(solution)/shard_map/ppermute | solution.py:31
  44.6 11.8 %collective-permute-start.6 = (bf16[3072,128]{1,0:T(8,128)(2,1)S(1)}, bf16[3072,128]{1,0:T(8,128)(2,1)S(1)}, u32[]{:S(2)}, u32[]{:S(2)}) collective-permute-start(bf16[3072,128]{1,0:T(8,128)(2,1)S(1)} %get-tuple-element.18.refs_2_), channel_id=1, source_target_pairs={{0,2},{2,4},{4,6},{1,3},{3,5},{5,7},{8,10},{10,12},{12,14},{9,11},... | collective-permute-start | bytes 2359304 | tf_op jit(solution)/shard_map/ppermute | solution.py:31
  46.0 14.1 %collective-permute-start.7 = (bf16[3072,128]{1,0:T(8,128)(2,1)S(1)}, bf16[3072,128]{1,0:T(8,128)(2,1)S(1)}, u32[]{:S(2)}, u32[]{:S(2)}) collective-permute-start(bf16[3072,128]{1,0:T(8,128)(2,1)S(1)} %get-tuple-element.18.refs_2_), channel_id=1, source_target_pairs={{2,0},{4,2},{6,4},{3,1},{5,3},{7,5},{10,8},{12,10},{14,12},{11,9},... | collective-permute-start | bytes 2359304 | tf_op jit(solution)/shard_map/ppermute | solution.py:31
  50.0 10.1 %collective-permute-start.9 = (bf16[1584,128]{1,0:T(8,128)(2,1)S(1)}, bf16[1584,128]{1,0:T(8,128)(2,1)S(1)}, u32[]{:S(2)}, u32[]{:S(2)}) collective-permute-start(bf16[1584,128]{1,0:T(8,128)(2,1)S(1)} %collective-permute-done.8.refs_0_), channel_id=1, source_target_pairs={{8,0},{16,8},{24,16},{32,24},{40,32},{48,40},{56,48},{64,56},{72,6... | collective-permute-start | bytes 1216520 | tf_op jit(solution)/shard_map/ppermute | solution.py:31
  55.0 21.2 %collective-permute-start.1 = (bf16[3072,128]{1,0:T(8,128)(2,1)S(1)}, bf16[3072,128]{1,0:T(8,128)(2,1)S(1)}, u32[]{:S(2)}, u32[]{:S(2)}) collective-permute-start(bf16[3072,128]{1,0:T(8,128)(2,1)S(1)} %collective-permute-done.refs_2_.refs_3_), channel_id=1, source_target_pairs={{8,16},{16,24},{24,32},{32,40},{40,48},{48,56},{56,64},{64,72},{72... | collective-permute-start | bytes 2359304 | tf_op jit(solution)/shard_map/ppermute | solution.py:31
  61.4 9.8 %collective-permute-start.10 = (bf16[1584,128]{1,0:T(8,128)(2,1)S(1)}, bf16[1584,128]{1,0:T(8,128)(2,1)S(1)}, u32[]{:S(2)}, u32[]{:S(2)}) collective-permute-start(bf16[1584,128]{1,0:T(8,128)(2,1)S(1)} %attend.9), channel_id=1, source_target_pairs={{0,8},{8,16},{16,24},{24,32},{32,40},{40,48},{48,56},{56,64},{64,7... | collective-permute-start | bytes 1216520 | tf_op jit(solution)/shard_map/ppermute | solution.py:31
  63.4 12.9 %collective-permute-start.2 = (bf16[1584,128]{1,0:T(8,128)(2,1)S(1)}, bf16[1584,128]{1,0:T(8,128)(2,1)S(1)}, u32[]{:S(2)}, u32[]{:S(2)}) collective-permute-start(bf16[1584,128]{1,0:T(8,128)(2,1)S(1)} %get-tuple-element.13.refs_0_), channel_id=1, source_target_pairs={{0,2},{2,4},{4,6},{1,3},{3,5},{5,7},{8,10},{10,12},{12,14},{9,11},... | collective-permute-start | bytes 1216520 | tf_op jit(solution)/shard_map/ppermute | solution.py:31
  65.5 10.7 %collective-permute-start.3 = (bf16[1584,128]{1,0:T(8,128)(2,1)S(1)}, bf16[1584,128]{1,0:T(8,128)(2,1)S(1)}, u32[]{:S(2)}, u32[]{:S(2)}) collective-permute-start(bf16[1584,128]{1,0:T(8,128)(2,1)S(1)} %get-tuple-element.13.refs_0_), channel_id=1, source_target_pairs={{2,0},{4,2},{6,4},{3,1},{5,3},{7,5},{10,8},{12,10},{14,12},{11,9},... | collective-permute-start | bytes 1216520 | tf_op jit(solution)/shard_map/ppermute | solution.py:31
  71.4 14.5 %collective-permute-start.11 = (bf16[1584,128]{1,0:T(8,128)(2,1)S(1)}, bf16[1584,128]{1,0:T(8,128)(2,1)S(1)}, u32[]{:S(2)}, u32[]{:S(2)}) collective-permute-start(bf16[1584,128]{1,0:T(8,128)(2,1)S(1)} %merge.1), channel_id=1, source_target_pairs={{0,8},{8,16},{16,24},{24,32},{32,40},{40,48},{48,56},{56,64},{64,7... | collective-permute-start | bytes 1216520 | tf_op jit(solution)/shard_map/ppermute | solution.py:31
  77.8 9.5 %collective-permute-start.4 = (bf16[1584,128]{1,0:T(8,128)(2,1)S(1)}, bf16[1584,128]{1,0:T(8,128)(2,1)S(1)}, u32[]{:S(2)}, u32[]{:S(2)}) collective-permute-start(bf16[1584,128]{1,0:T(8,128)(2,1)S(1)} %get-tuple-element.15), channel_id=1, source_target_pairs={{0,2},{2,4},{4,6},{1,3},{3,5},{5,7},{8,10},{10,12},{12,14},{9,11},... | collective-permute-start | bytes 1216520 | tf_op jit(solution)/shard_map/ppermute | solution.py:31
  81.9 9.8 %collective-permute-start.5 = (bf16[1584,128]{1,0:T(8,128)(2,1)S(1)}, bf16[1584,128]{1,0:T(8,128)(2,1)S(1)}, u32[]{:S(2)}, u32[]{:S(2)}) collective-permute-start(bf16[1584,128]{1,0:T(8,128)(2,1)S(1)} %get-tuple-element.16), channel_id=1, source_target_pairs={{2,0},{4,2},{6,4},{3,1},{5,3},{7,5},{10,8},{12,10},{14,12},{11,9},... | collective-permute-start | bytes 1216520 | tf_op jit(solution)/shard_map/ppermute | solution.py:31

commit v3 on v2

--- a/solution.py
+++ b/solution.py
@@ -293,17 +293,6 @@
             piece = side_by_side(ref, j * tokens, tokens).astype(jnp.float32)
             out = out + piece * share[j : j + 1, :]
         write(j, out.astype(jnp.bfloat16))
-    return jnp.where(top > 0.5 * NEVER, top + jnp.log2(total), NEVER)
-
-
-def merge_kernel(heads, tokens, checks, ok_ref, local, *refs):
-    priors, out_ref = refs[:-1], refs[-1]
-
-    def write(j, out):
-        write_partial(out_ref, heads, tokens, [(j, out)], None)
-
-    lse = merged(heads, tokens, ok_ref, local, priors, checks, write)
-    write_partial(out_ref, heads, tokens, [], lse)
 
 
 def finish_kernel(heads, tokens, cols, parts, ok_ref, *refs):
@@ -326,21 +315,6 @@
         merged(heads, tokens, ok_ref, local, priors, checks, write)
     for copy in copies:
         copy.wait()
-
-
-def merge(heads, shape, ok, local, priors, checks):
-    tokens = shape[0] * shape[1]
-    return pl.pallas_call(
-        functools.partial(merge_kernel, heads, tokens, checks),
-        out_shape=partial_shape(heads, tokens),
-        in_specs=[WHOLE] * (2 + len(priors)),
-        out_specs=WHOLE,
-        compiler_params=pltpu.CompilerParams(vmem_limit_bytes=8 * 2**20),
-        cost_estimate=pl.CostEstimate(
-            flops=10**8, bytes_accessed=8 * heads * tokens * HDIM, transcendentals=0
-        ),
-        name="merge",
-    )(ok, local, *priors)
 
 
 def finish(heads, shape, ok, *parts):
@@ -406,14 +380,13 @@
     offsets = [tuple(3 * back + dy for dy in range(3)) for back in range(3)]
 
     (k2,) = go((offsets[2],), (True,), row_cases, qs=(q2,), kvs=across)
-    p2 = shift(k2, "tm", 1, ahead=1)
-    (k1,) = go((offsets[1],), mine, row_cases, qs=(q1,), kvs=across)
+    p2 = shift(k2, "tm", 2)
+    (k1,) = go((offsets[1],), (True,), row_cases, qs=(q1,), kvs=across)
+    p1 = shift(k1, "tm", 1)
     (k0,) = go((offsets[0],), mine, row_cases, qs=(qb,), kvs=across)
-    m1 = merge(half, shape, ok, k1, (p2,), (FRAME_1,))
-    p1 = shift(m1, "tm", 1)
 
     part_a = (0, ka, (pm, pp), (ROW_BEFORE, ROW_AFTER))
-    part_b = (half, k0, (p1,), (FRAME_1,))
+    part_b = (half, k0, (p1, p2), (FRAME_1, FRAME_2))
     return finish(half, shape, ok, part_a, part_b)
 
 

time: 93.6 us -> 89.2 us (0.953)
  the two profiles are of different devices: /device:TPU:160 before, /device:TPU:288 now
where the time goes in v3:
time: 89.2 us; the launch traced here: 88.7 us
  starting transfers between devices  55.9 us (63%)
  waiting for transfers between devices  20.1 us (23%)
  Pallas kernels  12.4 us (14%)
    ppermute x12, starting transfers between devices, shift(): return lax.ppermute(block, axis, route)  55.9 us
    ppermute x12, waiting for transfers between devices, shift(): return lax.ppermute(block, axis, route)  20.1 us
    pallas_call x5, Pallas kernels, attend(): pl.pallas_call(functools.partial(attend_kernel, heads, tokens, cols, sets...  9.11 us
    pallas_call x1, Pallas kernels, pack(): pl.pallas_call(functools.partial(pack_kernel, heads, tokens), out_shape=s...  2.04 us
  transfers between devices with their start and end apart: 12, of which 4 were waited for; matrix products, arithmetic and copies ran while one was open for 0% of the time, Pallas kernels for 10%

profile of v3, /device:TPU:288, one launch (start us, length us, event | category | flops | bytes accessed | tf_op | source)
XLA Modules:
  0.0 88.7 jit_solution(12465880753653700056)
XLA Ops:
  0.0 2.0 %pack.1 = (bf16[1584,128]{1,0:T(8,128)(2,1)S(1)}, bf16[3072,128]{1,0:T(8,128)(2,1)S(1)}, bf16[1584,128]{1,0:T(8,128)(2,1)S(1)}, bf16[3072,128]{1,0:T(8,128)(2,1)S(1)}, s32[8,128]{1,0:T(8,128)S(1)}) custom-call(bf16[1,8,32,1536]{3,2,1,0:T(8,128)(2,1)} %q_ref.1, bf16[1,8,32,1536]{3,2,1,0:T(8,128)(2,1)} %k_ref.1, bf16[1,8,32,1536]{3,2,1,0:T(8,128)(2,1)} %v_ref.1, ...), custom_call_target="tpu_custom_call" | custom-call | flops 1000000000 | bytes 2359296 | tf_op jit(solution)/shard_map/pack/pallas_call | solution.py:107
  2.0 4.7 %collective-permute-start = (bf16[3072,128]{1,0:T(8,128)(2,1)S(1)}, bf16[3072,128]{1,0:T(8,128)(2,1)S(1)}, u32[]{:S(2)}, u32[]{:S(2)}) collective-permute-start(bf16[3072,128]{1,0:T(8,128)(2,1)S(1)} %get-tuple-element.14.refs_1_.refs_2_), channel_id=1, source_target_pairs={{0,8},{8,16},{16,24},{24,32},{32,40},{40,48},{48,56},{56,64},{64,7... | collective-permute-start | bytes 2359304 | tf_op jit(solution)/shard_map/ppermute | solution.py:31
  6.8 3.6 %collective-permute-start.6 = (bf16[3072,128]{1,0:T(8,128)(2,1)S(1)}, bf16[3072,128]{1,0:T(8,128)(2,1)S(1)}, u32[]{:S(2)}, u32[]{:S(2)}) collective-permute-start(bf16[3072,128]{1,0:T(8,128)(2,1)S(1)} %get-tuple-element.18.refs_2_), channel_id=1, source_target_pairs={{0,2},{2,4},{4,6},{1,3},{3,5},{5,7},{8,10},{10,12},{12,14},{9,11},... | collective-permute-start | bytes 2359304 | tf_op jit(solution)/shard_map/ppermute | solution.py:31
  10.4 1.3 %collective-permute-start.7 = (bf16[3072,128]{1,0:T(8,128)(2,1)S(1)}, bf16[3072,128]{1,0:T(8,128)(2,1)S(1)}, u32[]{:S(2)}, u32[]{:S(2)}) collective-permute-start(bf16[3072,128]{1,0:T(8,128)(2,1)S(1)} %get-tuple-element.18.refs_2_), channel_id=1, source_target_pairs={{2,0},{4,2},{6,4},{3,1},{5,3},{7,5},{10,8},{12,10},{14,12},{11,9},... | collective-permute-start | bytes 2359304 | tf_op jit(solution)/shard_map/ppermute | solution.py:31
  11.7 2.0 %collective-permute-start.8 = (bf16[1584,128]{1,0:T(8,128)(2,1)S(1)}, bf16[1584,128]{1,0:T(8,128)(2,1)S(1)}, u32[]{:S(2)}, u32[]{:S(2)}) collective-permute-start(bf16[1584,128]{1,0:T(8,128)(2,1)S(1)} %get-tuple-element.17.refs_0_), channel_id=1, source_target_pairs={{8,0},{16,8},{24,16},{32,24},{40,32},{48,40},{56,48},{64,56},{72,6... | collective-permute-start | bytes 1216520 | tf_op jit(solution)/shard_map/ppermute | solution.py:31
  13.7 10.7 %collective-permute-done.refs_2_.refs_3_ = bf16[3072,128]{1,0:T(8,128)(2,1)S(1)} collective-permute-done((bf16[3072,128]{1,0:T(8,128)(2,1)S(1)}, bf16[3072,128]{1,0:T(8,128)(2,1)S(1)}, u32[]{:S(2)}, u32[]{:S(2)}) %collective-permute-start) | collective-permute-done | bytes 786464 | tf_op jit(solution)/shard_map/ppermute | solution.py:31
  24.3 5.7 %collective-permute-start.1 = (bf16[3072,128]{1,0:T(8,128)(2,1)S(1)}, bf16[3072,128]{1,0:T(8,128)(2,1)S(1)}, u32[]{:S(2)}, u32[]{:S(2)}) collective-permute-start(bf16[3072,128]{1,0:T(8,128)(2,1)S(1)} %collective-permute-done.refs_2_.refs_3_), channel_id=1, source_target_pairs={{8,16},{16,24},{24,32},{32,40},{40,48},{48,56},{56,64},{64,72},{72... | collective-permute-start | bytes 2359304 | tf_op jit(solution)/shard_map/ppermute | solution.py:31
  30.1 0.0 collective-permute-done.8.refs_0_
  30.1 27.2 %collective-permute-start.10 = (bf16[1584,128]{1,0:T(8,128)(2,1)S(1)}, bf16[1584,128]{1,0:T(8,128)(2,1)S(1)}, u32[]{:S(2)}, u32[]{:S(2)}) collective-permute-start(bf16[1584,128]{1,0:T(8,128)(2,1)S(1)} %collective-permute-done.8.refs_0_), channel_id=1, source_target_pairs={{8,0},{16,8},{24,16},{32,24},{40,32},{48,40},{56,48},{64,56},{72,6... | collective-permute-start | bytes 1216520 | tf_op jit(solution)/shard_map/ppermute | solution.py:31
  57.3 1.3 %collective-permute-start.2 = (bf16[1584,128]{1,0:T(8,128)(2,1)S(1)}, bf16[1584,128]{1,0:T(8,128)(2,1)S(1)}, u32[]{:S(2)}, u32[]{:S(2)}) collective-permute-start(bf16[1584,128]{1,0:T(8,128)(2,1)S(1)} %get-tuple-element.13.refs_0_), channel_id=1, source_target_pairs={{0,2},{2,4},{4,6},{1,3},{3,5},{5,7},{8,10},{10,12},{12,14},{9,11},... | collective-permute-start | bytes 1216520 | tf_op jit(solution)/shard_map/ppermute | solution.py:31
  58.6 1.3 %collective-permute-start.3 = (bf16[1584,128]{1,0:T(8,128)(2,1)S(1)}, bf16[1584,128]{1,0:T(8,128)(2,1)S(1)}, u32[]{:S(2)}, u32[]{:S(2)}) collective-permute-start(bf16[1584,128]{1,0:T(8,128)(2,1)S(1)} %get-tuple-element.13.refs_0_), channel_id=1, source_target_pairs={{2,0},{4,2},{6,4},{3,1},{5,3},{7,5},{10,8},{12,10},{14,12},{11,9},... | collective-permute-start | bytes 1216520 | tf_op jit(solution)/shard_map/ppermute | solution.py:31
  60.0 1.3 %attend.8 = bf16[1584,128]{1,0:T(8,128)(2,1)S(1)} custom-call(bf16[1584,128]{1,0:T(8,128)(2,1)S(1)} %collective-permute-done.8.refs_0_, bf16[3072,128]{1,0:T(8,128)(2,1)S(1)} %collective-permute-done.6.refs_1_, bf16[3072,128]{1,0:T(8,128)(2,1)S(1)} %get-tuple-element.18.refs_2_, bf16[3072,128]{1,0:T(8,128)(2,1)S(1)} %collective-permute-done.7.refs_3_), custom_call_target="tpu_custom_call" | custom-call | flops 1000000000 | bytes 1572864 | tf_op jit(solution)/shard_map/attend/pallas_call | solution.py:268
  61.3 2.0 %collective-permute-start.9 = (bf16[1584,128]{1,0:T(8,128)(2,1)S(1)}, bf16[1584,128]{1,0:T(8,128)(2,1)S(1)}, u32[]{:S(2)}, u32[]{:S(2)}) collective-permute-start(bf16[1584,128]{1,0:T(8,128)(2,1)S(1)} %attend.8), channel_id=1, source_target_pairs={{0,8},{8,16},{16,24},{24,32},{32,40},{40,48},{48,56},{56,64},{64,7... | collective-permute-start | bytes 1216520 | tf_op jit(solution)/shard_map/ppermute | solution.py:31
  63.2 1.3 %attend.9 = bf16[1584,128]{1,0:T(8,128)(2,1)S(1)} custom-call(bf16[1584,128]{1,0:T(8,128)(2,1)S(1)} %collective-permute-done.10.refs_0_, bf16[3072,128]{1,0:T(8,128)(2,1)S(1)} %collective-permute-done.6.refs_1_, bf16[3072,128]{1,0:T(8,128)(2,1)S(1)} %get-tuple-element.18.refs_2_, bf16[3072,128]{1,0:T(8,128)(2,1)S(1)} %collective-permute-done.7.refs_3_), custom_call_target="tpu_custom_call" | custom-call | flops 1000000000 | bytes 1572864 | tf_op jit(solution)/shard_map/attend/pallas_call | solution.py:268
  64.6 2.0 %collective-permute-start.11 = (bf16[1584,128]{1,0:T(8,128)(2,1)S(1)}, bf16[1584,128]{1,0:T(8,128)(2,1)S(1)}, u32[]{:S(2)}, u32[]{:S(2)}) collective-permute-start(bf16[1584,128]{1,0:T(8,128)(2,1)S(1)} %attend.9), channel_id=1, source_target_pairs={{0,16},{8,24},{16,32},{24,40},{32,48},{40,56},{48,64},{56,72},{64,... | collective-permute-start | bytes 1216520 | tf_op jit(solution)/shard_map/ppermute | solution.py:31
  66.5 4.0 %collective-permute-done.3.refs_1_ = bf16[1584,128]{1,0:T(8,128)(2,1)S(1)} collective-permute-done((bf16[1584,128]{1,0:T(8,128)(2,1)S(1)}, bf16[1584,128]{1,0:T(8,128)(2,1)S(1)}, u32[]{:S(2)}, u32[]{:S(2)}) %collective-permute-start.3) | collective-permute-done | bytes 405536 | tf_op jit(solution)/shard_map/ppermute | solution.py:31
  70.6 3.3 %attend.6 = (bf16[1584,128]{1,0:T(8,128)(2,1)S(1)}, bf16[1584,128]{1,0:T(8,128)(2,1)S(1)}) custom-call(bf16[1584,128]{1,0:T(8,128)(2,1)S(1)} %collective-permute-done.2.refs_0_, bf16[1584,128]{1,0:T(8,128)(2,1)S(1)} %collective-permute-done.3.refs_1_, bf16[3072,128]{1,0:T(8,128)(2,1)S(1)} %get-tuple-element.14.refs_1_.refs_2_, ...), custom_call_target="tpu_custom_call" | custom-call | flops 1000000000 | bytes 1572864 | tf_op jit(solution)/shard_map/attend/pallas_call | solution.py:268
  73.9 3.5 %collective-permute-start.4 = (bf16[1584,128]{1,0:T(8,128)(2,1)S(1)}, bf16[1584,128]{1,0:T(8,128)(2,1)S(1)}, u32[]{:S(2)}, u32[]{:S(2)}) collective-permute-start(bf16[1584,128]{1,0:T(8,128)(2,1)S(1)} %get-tuple-element.15), channel_id=1, source_target_pairs={{0,2},{2,4},{4,6},{1,3},{3,5},{5,7},{8,10},{10,12},{12,14},{9,11},... | collective-permute-start | bytes 1216520 | tf_op jit(solution)/shard_map/ppermute | solution.py:31
  77.5 1.3 %collective-permute-start.5 = (bf16[1584,128]{1,0:T(8,128)(2,1)S(1)}, bf16[1584,128]{1,0:T(8,128)(2,1)S(1)}, u32[]{:S(2)}, u32[]{:S(2)}) collective-permute-start(bf16[1584,128]{1,0:T(8,128)(2,1)S(1)} %get-tuple-element.16), channel_id=1, source_target_pairs={{2,0},{4,2},{6,4},{3,1},{5,3},{7,5},{10,8},{12,10},{14,12},{11,9},... | collective-permute-start | bytes 1216520 | tf_op jit(solution)/shard_map/ppermute | solution.py:31
  78.8 1.3 %attend.7.refs_3_ = f32[776,256]{1,0:T(8,128)S(1)} custom-call(bf16[1584,128]{1,0:T(8,128)(2,1)S(1)} %get-tuple-element.17.refs_0_, bf16[3072,128]{1,0:T(8,128)(2,1)S(1)} %collective-permute-done.6.refs_1_, bf16[3072,128]{1,0:T(8,128)(2,1)S(1)} %get-tuple-element.18.refs_2_, bf16[3072,128]{1,0:T(8,128)(2,1)S(1)} %collective-permute-done.7.refs_3_), custom_call_target="tpu_custom_call" | custom-call | flops 1000000000 | bytes 1572864 | tf_op jit(solution)/shard_map/attend/pallas_call | solution.py:268
  80.1 1.8 %attend.5.refs_0_ = f32[776,256]{1,0:T(8,128)S(1)} custom-call(bf16[1584,128]{1,0:T(8,128)(2,1)S(1)} %get-tuple-element.13.refs_0_, bf16[3072,128]{1,0:T(8,128)(2,1)S(1)} %get-tuple-element.14.refs_1_.refs_2_, bf16[3072,128]{1,0:T(8,128)(2,1)S(1)} %collective-permute-done.refs_2_.refs_3_, bf16[3072,128]{1,0:T(8,128)(2,1)S(1)} %collective-permute-done.1.refs_3_.refs_4_), custom_call_target="tpu_custom_call" | custom-call | flops 1000000000 | bytes 1572864 | tf_op jit(solution)/shard_map/attend/pallas_call | solution.py:268
  81.9 0.9 collective-permute-done.4.refs_1_
  82.8 4.4 %collective-permute-done.5.refs_2_ = bf16[1584,128]{1,0:T(8,128)(2,1)S(1)} collective-permute-done((bf16[1584,128]{1,0:T(8,128)(2,1)S(1)}, bf16[1584,128]{1,0:T(8,128)(2,1)S(1)}, u32[]{:S(2)}, u32[]{:S(2)}) %collective-permute-start.5) | collective-permute-done | bytes 405536 | tf_op jit(solution)/shard_map/ppermute | solution.py:31
  87.3 1.3 %finish.1 = bf16[1,8,32,1536]{3,2,1,0:T(8,128)(2,1)} custom-call(s32[8,128]{1,0:T(8,128)S(1)} %get-tuple-element.12.ok_ref, f32[776,256]{1,0:T(8,128)S(1)} %attend.5.refs_0_, bf16[1584,128]{1,0:T(8,128)(2,1)S(1)} %collective-permute-done.4.refs_1_, bf16[1584,128]{1,0:T(8,128)(2,1)S(1)} %collective-permute-done.5.refs_2_, f32[776,256]{1,0:T(8,128)S(1)} %attend.7.refs_3_, ...), custom_call_target="tpu_custom_call" | custom-call | flops 100000000 | bytes 3145728 | tf_op jit(solution)/shard_map/finish/pallas_call | solution.py:327
  (7 shorter events, 0.0 us)
Async XLA Ops:
  2.0 22.3 %collective-permute-start = (bf16[3072,128]{1,0:T(8,128)(2,1)S(1)}, bf16[3072,128]{1,0:T(8,128)(2,1)S(1)}, u32[]{:S(2)}, u32[]{:S(2)}) collective-permute-start(bf16[3072,128]{1,0:T(8,128)(2,1)S(1)} %get-tuple-element.14.refs_1_.refs_2_), channel_id=1, source_target_pairs={{0,8},{8,16},{16,24},{24,32},{32,40},{40,48},{48,56},{56,64},{64,7... | collective-permute-start | bytes 2359304 | tf_op jit(solution)/shard_map/ppermute | solution.py:31
  6.8 51.8 %collective-permute-start.6 = (bf16[3072,128]{1,0:T(8,128)(2,1)S(1)}, bf16[3072,128]{1,0:T(8,128)(2,1)S(1)}, u32[]{:S(2)}, u32[]{:S(2)}) collective-permute-start(bf16[3072,128]{1,0:T(8,128)(2,1)S(1)} %get-tuple-element.18.refs_2_), channel_id=1, source_target_pairs={{0,2},{2,4},{4,6},{1,3},{3,5},{5,7},{8,10},{10,12},{12,14},{9,11},... | collective-permute-start | bytes 2359304 | tf_op jit(solution)/shard_map/ppermute | solution.py:31
  10.4 49.6 %collective-permute-start.7 = (bf16[3072,128]{1,0:T(8,128)(2,1)S(1)}, bf16[3072,128]{1,0:T(8,128)(2,1)S(1)}, u32[]{:S(2)}, u32[]{:S(2)}) collective-permute-start(bf16[3072,128]{1,0:T(8,128)(2,1)S(1)} %get-tuple-element.18.refs_2_), channel_id=1, source_target_pairs={{2,0},{4,2},{6,4},{3,1},{5,3},{7,5},{10,8},{12,10},{14,12},{11,9},... | collective-permute-start | bytes 2359304 | tf_op jit(solution)/shard_map/ppermute | solution.py:31
  11.7 18.4 %collective-permute-start.8 = (bf16[1584,128]{1,0:T(8,128)(2,1)S(1)}, bf16[1584,128]{1,0:T(8,128)(2,1)S(1)}, u32[]{:S(2)}, u32[]{:S(2)}) collective-permute-start(bf16[1584,128]{1,0:T(8,128)(2,1)S(1)} %get-tuple-element.17.refs_0_), channel_id=1, source_target_pairs={{8,0},{16,8},{24,16},{32,24},{40,32},{48,40},{56,48},{64,56},{72,6... | collective-permute-start | bytes 1216520 | tf_op jit(solution)/shard_map/ppermute | solution.py:31
  24.3 46.2 %collective-permute-start.1 = (bf16[3072,128]{1,0:T(8,128)(2,1)S(1)}, bf16[3072,128]{1,0:T(8,128)(2,1)S(1)}, u32[]{:S(2)}, u32[]{:S(2)}) collective-permute-start(bf16[3072,128]{1,0:T(8,128)(2,1)S(1)} %collective-permute-done.refs_2_.refs_3_), channel_id=1, source_target_pairs={{8,16},{16,24},{24,32},{32,40},{40,48},{48,56},{56,64},{64,72},{72... | collective-permute-start | bytes 2359304 | tf_op jit(solution)/shard_map/ppermute | solution.py:31
  30.1 33.1 %collective-permute-start.10 = (bf16[1584,128]{1,0:T(8,128)(2,1)S(1)}, bf16[1584,128]{1,0:T(8,128)(2,1)S(1)}, u32[]{:S(2)}, u32[]{:S(2)}) collective-permute-start(bf16[1584,128]{1,0:T(8,128)(2,1)S(1)} %collective-permute-done.8.refs_0_), channel_id=1, source_target_pairs={{8,0},{16,8},{24,16},{32,24},{40,32},{48,40},{56,48},{64,56},{72,6... | collective-permute-start | bytes 1216520 | tf_op jit(solution)/shard_map/ppermute | solution.py:31
  57.3 9.3 %collective-permute-start.2 = (bf16[1584,128]{1,0:T(8,128)(2,1)S(1)}, bf16[1584,128]{1,0:T(8,128)(2,1)S(1)}, u32[]{:S(2)}, u32[]{:S(2)}) collective-permute-start(bf16[1584,128]{1,0:T(8,128)(2,1)S(1)} %get-tuple-element.13.refs_0_), channel_id=1, source_target_pairs={{0,2},{2,4},{4,6},{1,3},{3,5},{5,7},{8,10},{10,12},{12,14},{9,11},... | collective-permute-start | bytes 1216520 | tf_op jit(solution)/shard_map/ppermute | solution.py:31
  58.6 11.9 %collective-permute-start.3 = (bf16[1584,128]{1,0:T(8,128)(2,1)S(1)}, bf16[1584,128]{1,0:T(8,128)(2,1)S(1)}, u32[]{:S(2)}, u32[]{:S(2)}) collective-permute-start(bf16[1584,128]{1,0:T(8,128)(2,1)S(1)} %get-tuple-element.13.refs_0_), channel_id=1, source_target_pairs={{2,0},{4,2},{6,4},{3,1},{5,3},{7,5},{10,8},{12,10},{14,12},{11,9},... | collective-permute-start | bytes 1216520 | tf_op jit(solution)/shard_map/ppermute | solution.py:31
  61.3 20.7 %collective-permute-start.9 = (bf16[1584,128]{1,0:T(8,128)(2,1)S(1)}, bf16[1584,128]{1,0:T(8,128)(2,1)S(1)}, u32[]{:S(2)}, u32[]{:S(2)}) collective-permute-start(bf16[1584,128]{1,0:T(8,128)(2,1)S(1)} %attend.8), channel_id=1, source_target_pairs={{0,8},{8,16},{16,24},{24,32},{32,40},{40,48},{48,56},{56,64},{64,7... | collective-permute-start | bytes 1216520 | tf_op jit(solution)/shard_map/ppermute | solution.py:31
  64.6 17.4 %collective-permute-start.11 = (bf16[1584,128]{1,0:T(8,128)(2,1)S(1)}, bf16[1584,128]{1,0:T(8,128)(2,1)S(1)}, u32[]{:S(2)}, u32[]{:S(2)}) collective-permute-start(bf16[1584,128]{1,0:T(8,128)(2,1)S(1)} %attend.9), channel_id=1, source_target_pairs={{0,16},{8,24},{16,32},{24,40},{32,48},{40,56},{48,64},{56,72},{64,... | collective-permute-start | bytes 1216520 | tf_op jit(solution)/shard_map/ppermute | solution.py:31
  73.9 8.9 %collective-permute-start.4 = (bf16[1584,128]{1,0:T(8,128)(2,1)S(1)}, bf16[1584,128]{1,0:T(8,128)(2,1)S(1)}, u32[]{:S(2)}, u32[]{:S(2)}) collective-permute-start(bf16[1584,128]{1,0:T(8,128)(2,1)S(1)} %get-tuple-element.15), channel_id=1, source_target_pairs={{0,2},{2,4},{4,6},{1,3},{3,5},{5,7},{8,10},{10,12},{12,14},{9,11},... | collective-permute-start | bytes 1216520 | tf_op jit(solution)/shard_map/ppermute | solution.py:31
  77.5 9.8 %collective-permute-start.5 = (bf16[1584,128]{1,0:T(8,128)(2,1)S(1)}, bf16[1584,128]{1,0:T(8,128)(2,1)S(1)}, u32[]{:S(2)}, u32[]{:S(2)}) collective-permute-start(bf16[1584,128]{1,0:T(8,128)(2,1)S(1)} %get-tuple-element.16), channel_id=1, source_target_pairs={{2,0},{4,2},{6,4},{3,1},{5,3},{7,5},{10,8},{12,10},{14,12},{11,9},... | collective-permute-start | bytes 1216520 | tf_op jit(solution)/shard_map/ppermute | solution.py:31

commit v4 on v3

--- a/solution.py
+++ b/solution.py
@@ -1,4 +1,5 @@
 import functools
+import itertools
 
 import jax
 import jax.numpy as jnp
@@ -29,6 +30,16 @@
         if 0 <= i + by < size and i + by + ahead < size and i + ahead < size
     ]
     return lax.ppermute(block, axis, route)
+
+
+def hop(block, axes, by, pick):
+    sizes = [lax.axis_size(axis) for axis in axes]
+    route = []
+    for place in itertools.product(*map(range, sizes)):
+        to = [p + b for p, b in zip(place, by)]
+        if pick(place) and all(0 <= t < n for t, n in zip(to, sizes)):
+            route.append((place[0] * sizes[1] + place[1], to[0] * sizes[1] + to[1]))
+    return lax.ppermute(block, axes, route)
 
 
 def masks(tcols, flags, window):
@@ -171,6 +182,8 @@
             run(chosen, used)
             return
         pl.when(hit)(functools.partial(run, chosen, used))
+        if not where:
+            return
         rest = jnp.logical_not(hit) if rest is None else rest & jnp.logical_not(hit)
 
 
@@ -238,17 +251,16 @@
                 out = outs.pop(key) * (1.0 / jnp.maximum(total, 1e-30))
                 lse = tops[key] + jnp.log2(total)
                 lses[which] = jnp.where((sub == j) & (total > 0), lse, lses[which])
-                if packed[which]:
-                    write_partial(
-                        out_refs[which], heads, tokens, [(j, out.astype(jnp.bfloat16))], None
-                    )
+                if packed[which % len(packed)]:
+                    piece = [(j, out.astype(jnp.bfloat16))]
+                    write_partial(out_refs[which % len(out_refs)], heads, tokens, piece, None)
                 else:
-                    out_refs[which][j * HDIM : (j + 1) * HDIM, :] = out
+                    out_refs[which % len(out_refs)][j * HDIM : (j + 1) * HDIM, :] = out
     for which, lse in lses.items():
-        if packed[which]:
-            write_partial(out_refs[which], heads, tokens, [], lse)
+        if packed[which % len(packed)]:
+            write_partial(out_refs[which % len(out_refs)], heads, tokens, [], lse)
         else:
-            out_refs[which][heads * HDIM :, :] = lse
+            out_refs[which % len(out_refs)][heads * HDIM :, :] = lse
 
 
 def partial_shape(heads, tokens):
@@ -295,47 +307,49 @@
         write(j, out.astype(jnp.bfloat16))
 
 
-def finish_kernel(heads, tokens, cols, parts, ok_ref, *refs):
+def finish_kernel(heads, tokens, cols, first, checks, ok_ref, local, *refs):
+    priors = refs[: len(checks)]
     out_ref, stage, sems = refs[-3:]
     copies = []
-    for first, checks in parts:
-        local, priors, refs = refs[0], refs[1 : 1 + len(checks)], refs[1 + len(checks) :]
-
-        def write(j, out):
-            at = pl.ds((first + j) * tokens, tokens)
-            stage[at, :] = out.T
-            copy = pltpu.make_async_copy(
-                stage.at[at].reshape(tokens // cols, cols, HDIM),
-                out_ref.at[0, :, :, pl.ds((first + j) * HDIM, HDIM)],
-                sems.at[first + j],
-            )
-            copy.start()
-            copies.append(copy)
-
-        merged(heads, tokens, ok_ref, local, priors, checks, write)
+
+    def write(j, out):
+        at = pl.ds(j * tokens, tokens)
+        stage[at, :] = out.T
+        copy = pltpu.make_async_copy(
+            stage.at[at].reshape(tokens // cols, cols, HDIM),
+            out_ref.at[0, :, :, pl.ds((first + j) * HDIM, HDIM)],
+            sems.at[j],
+        )
+        copy.start()
+        copies.append(copy)
+
+    merged(heads, tokens, ok_ref, local, priors, checks, write)
     for copy in copies:
         copy.wait()
 
 
-def finish(heads, shape, ok, *parts):
+def finish(heads, shape, ok, first, local, priors, checks, into=None):
     rows, cols, channels = shape
     tokens = rows * cols
-    args = [ok]
-    for _, local, priors, _ in parts:
-        args += [local, *priors]
-    layout = tuple((first, checks) for first, _, _, checks in parts)
+    args, aliases = [ok, local, *priors], {}
+    specs = [WHOLE] * len(args)
+    if into is not None:
+        aliases = {len(args): 0}
+        args.append(into)
+        specs.append(pl.BlockSpec(memory_space=pl.ANY))
     return pl.pallas_call(
-        functools.partial(finish_kernel, heads, tokens, cols, layout),
+        functools.partial(finish_kernel, heads, tokens, cols, first, checks),
         out_shape=jax.ShapeDtypeStruct((1, rows, cols, channels), jnp.bfloat16),
-        in_specs=[WHOLE] * len(args),
+        in_specs=specs,
         out_specs=pl.BlockSpec(memory_space=pl.ANY),
+        input_output_aliases=aliases,
         scratch_shapes=[
-            pltpu.VMEM((tokens * channels // HDIM, HDIM), jnp.bfloat16),
-            pltpu.SemaphoreType.DMA((channels // HDIM,)),
+            pltpu.VMEM((heads * tokens, HDIM), jnp.bfloat16),
+            pltpu.SemaphoreType.DMA((heads,)),
         ],
         compiler_params=pltpu.CompilerParams(vmem_limit_bytes=8 * 2**20),
         cost_estimate=pl.CostEstimate(
-            flops=10**8, bytes_accessed=16 * heads * tokens * HDIM, transcendentals=0
+            flops=10**8, bytes_accessed=8 * heads * tokens * HDIM, transcendentals=0
         ),
         name="finish",
     )(*args)
@@ -366,28 +380,38 @@
         ((second,), (0, 1), (0, 1)),
     )
     frame_cases = (((first,), (0,), (0,)), ((second,), (0,), (0, 1)))
-    row_cases = (((edge,), (0,), (1, 2)), ((("space", -1),), (0,), (0, 1)))
     km, kp = go((frames[2], frames[0]), both, pair_cases, qs=(qm, qp), kvs=along)
     pp = shift(km, "space", -1)
     pm = shift(kp, "space", 1)
     (ka,) = go((frames[1],), mine, frame_cases, qs=(qa,), kvs=along)
 
-    q1 = shift(qb, "tm", -1)
+    grid = ("tm", "space")
+    below, beside = (1, 0), (0, 1)
+    q1 = hop(qb, grid, (-1, 0), lambda place: place != below)
+    q1_late = hop(qb, grid, (-1, 0), lambda place: place == below)
+    hi = hop(kvb, grid, (0, -1), lambda place: place != beside)
+    hi_late = hop(kvb, grid, (0, -1), lambda place: place == beside)
     q2 = shift(q1, "tm", -1, ahead=1)
     lo = shift(kvb, "space", 1)
-    hi = shift(kvb, "space", -1)
-    across = (lo, kvb, hi)
-    offsets = [tuple(3 * back + dy for dy in range(3)) for back in range(3)]
-
-    (k2,) = go((offsets[2],), (True,), row_cases, qs=(q2,), kvs=across)
+    across = (lo, kvb, hi, hi_late)
+    offsets = [tuple(3 * back + dy for dy in (0, 1, 2, 2)) for back in range(3)]
+
+    def row_cases(late=0):
+        return (
+            ((first, edge), (late,), (1, 3)),
+            ((edge,), (0,), (1, 2)),
+            ((("space", -1),), (0,), (0, 1)),
+            ((), (0,), (0, 1, 2)),
+        )
+
+    (k2,) = go((offsets[2],), (True,), row_cases(), qs=(q2,), kvs=across)
     p2 = shift(k2, "tm", 2)
-    (k1,) = go((offsets[1],), (True,), row_cases, qs=(q1,), kvs=across)
+    (k1,) = go((offsets[1],) * 2, (True,), row_cases(1), qs=(q1, q1_late), kvs=across)
     p1 = shift(k1, "tm", 1)
-    (k0,) = go((offsets[0],), mine, row_cases, qs=(qb,), kvs=across)
-
-    part_a = (0, ka, (pm, pp), (ROW_BEFORE, ROW_AFTER))
-    part_b = (half, k0, (p1, p2), (FRAME_1, FRAME_2))
-    return finish(half, shape, ok, part_a, part_b)
+    (k0,) = go((offsets[0],), mine, row_cases(), qs=(qb,), kvs=across)
+
+    out = finish(half, shape, ok, half, k0, (p1, p2), (FRAME_1, FRAME_2))
+    return finish(half, shape, ok, 0, ka, (pm, pp), (ROW_BEFORE, ROW_AFTER), into=out)
 
 
 def solution(mesh):

time: 89.2 us -> 88.4 us (level)
  the two profiles are of different devices: /device:TPU:288 before, /device:TPU:34 now
where the time goes in v4:
time: 88.4 us; the launch traced here: 87.9 us
  starting transfers between devices  69 us (78%)
  Pallas kernels  12.2 us (14%)
  waiting for transfers between devices  6.34 us (7%)
    ppermute x4, starting transfers between devices, hop(): return lax.ppermute(block, axes, route)  38.9 us
    ppermute x10, starting transfers between devices, shift(): return lax.ppermute(block, axis, route)  30.2 us
    pallas_call x5, Pallas kernels, attend(): pl.pallas_call(functools.partial(attend_kernel, heads, tokens, cols, sets...  8.16 us
    ppermute x10, waiting for transfers between devices, shift(): return lax.ppermute(block, axis, route)  6.33 us
    pallas_call x1, Pallas kernels, pack(): pl.pallas_call(functools.partial(pack_kernel, heads, tokens), out_shape=s...  2.04 us
    pallas_call x2, Pallas kernels, finish(): pl.pallas_call(functools.partial(finish_kernel, heads, tokens, cols, firs...  1.98 us
  transfers between devices with their start and end apart: 14, of which 2 were waited for; matrix products, arithmetic and copies ran while one was open for 0% of the time, Pallas kernels for 10%

profile of v4, /device:TPU:34, one launch (start us, length us, event | category | flops | bytes accessed | tf_op | source)
XLA Modules:
  0.0 87.9 jit_solution(3277411676694314146)
XLA Ops:
  0.0 2.0 %pack.1 = (bf16[1584,128]{1,0:T(8,128)(2,1)S(1)}, bf16[3072,128]{1,0:T(8,128)(2,1)S(1)}, bf16[1584,128]{1,0:T(8,128)(2,1)S(1)}, bf16[3072,128]{1,0:T(8,128)(2,1)S(1)}, s32[8,128]{1,0:T(8,128)S(1)}) custom-call(bf16[1,8,32,1536]{3,2,1,0:T(8,128)(2,1)} %q_ref.1, bf16[1,8,32,1536]{3,2,1,0:T(8,128)(2,1)} %k_ref.1, bf16[1,8,32,1536]{3,2,1,0:T(8,128)(2,1)} %v_ref.1, ...), custom_call_target="tpu_custom_call" | custom-call | flops 1000000000 | bytes 2359296 | tf_op jit(solution)/shard_map/pack/pallas_call | solution.py:118
  2.0 4.8 %collective-permute-start = (bf16[3072,128]{1,0:T(8,128)(2,1)S(1)}, bf16[3072,128]{1,0:T(8,128)(2,1)S(1)}, u32[]{:S(2)}, u32[]{:S(2)}) collective-permute-start(bf16[3072,128]{1,0:T(8,128)(2,1)S(1)} %get-tuple-element.14.refs_1_.refs_2_), channel_id=1, source_target_pairs={{0,8},{8,16},{16,24},{24,32},{32,40},{40,48},{48,56},{56,64},{64,7... | collective-permute-start | bytes 2359304 | tf_op jit(solution)/shard_map/ppermute | solution.py:32
  6.8 1.3 %collective-permute-start.9 = (bf16[1584,128]{1,0:T(8,128)(2,1)S(1)}, bf16[1584,128]{1,0:T(8,128)(2,1)S(1)}, u32[]{:S(2)}, u32[]{:S(2)}) collective-permute-start(bf16[1584,128]{1,0:T(8,128)(2,1)S(1)} %get-tuple-element.17.refs_0_), channel_id=1, source_target_pairs={{10,2},{12,4},{14,6},{16,8},{18,10},{20,12},{22,14},{24,16},{26,18... | collective-permute-start | bytes 1216520 | tf_op jit(solution)/shard_map/ppermute | solution.py:42
  8.1 3.6 %collective-permute-start.6 = (bf16[3072,128]{1,0:T(8,128)(2,1)S(1)}, bf16[3072,128]{1,0:T(8,128)(2,1)S(1)}, u32[]{:S(2)}, u32[]{:S(2)}) collective-permute-start(bf16[3072,128]{1,0:T(8,128)(2,1)S(1)} %get-tuple-element.18.refs_2_.refs_3_), channel_id=1, source_target_pairs={{0,2},{2,4},{4,6},{1,3},{3,5},{5,7},{8,10},{10,12},{12,14},{9,11},... | collective-permute-start | bytes 2359304 | tf_op jit(solution)/shard_map/ppermute | solution.py:32
  11.7 1.3 %collective-permute-start.7 = (bf16[3072,128]{1,0:T(8,128)(2,1)S(1)}, bf16[3072,128]{1,0:T(8,128)(2,1)S(1)}, u32[]{:S(2)}, u32[]{:S(2)}) collective-permute-start(bf16[3072,128]{1,0:T(8,128)(2,1)S(1)} %get-tuple-element.18.refs_2_.refs_3_), channel_id=1, source_target_pairs={{4,2},{6,4},{10,8},{12,10},{14,12},{18,16},{20,18},{22,20},{26,24}... | collective-permute-start | bytes 2359304 | tf_op jit(solution)/shard_map/ppermute | solution.py:42
  13.0 35.6 %collective-permute-start.8 = (bf16[3072,128]{1,0:T(8,128)(2,1)S(1)}, bf16[3072,128]{1,0:T(8,128)(2,1)S(1)}, u32[]{:S(2)}, u32[]{:S(2)}) collective-permute-start(bf16[3072,128]{1,0:T(8,128)(2,1)S(1)} %get-tuple-element.18.refs_2_.refs_3_), channel_id=1, source_target_pairs={{2,0},{3,1},{258,256},{259,257}} | collective-permute-start | bytes 2359304 | tf_op jit(solution)/shard_map/ppermute | solution.py:42
  48.6 0.7 collective-permute-start.10
  49.3 0.7 collective-permute-start.1
  50.0 1.3 %collective-permute-start.12 = (bf16[1584,128]{1,0:T(8,128)(2,1)S(1)}, bf16[1584,128]{1,0:T(8,128)(2,1)S(1)}, u32[]{:S(2)}, u32[]{:S(2)}) collective-permute-start(bf16[1584,128]{1,0:T(8,128)(2,1)S(1)} %collective-permute-done.9.refs_0_), channel_id=1, source_target_pairs={{8,0},{16,8},{24,16},{32,24},{40,32},{48,40},{56,48},{64,56},{72,6... | collective-permute-start | bytes 1216520 | tf_op jit(solution)/shard_map/ppermute | solution.py:32
  51.3 4.4 %collective-permute-done.6.refs_1_.refs_2_ = bf16[3072,128]{1,0:T(8,128)(2,1)S(1)} collective-permute-done((bf16[3072,128]{1,0:T(8,128)(2,1)S(1)}, bf16[3072,128]{1,0:T(8,128)(2,1)S(1)}, u32[]{:S(2)}, u32[]{:S(2)}) %collective-permute-start.6) | collective-permute-done | bytes 786464 | tf_op jit(solution)/shard_map/ppermute | solution.py:32
  55.8 1.9 %collective-permute-start.2 = (bf16[1584,128]{1,0:T(8,128)(2,1)S(1)}, bf16[1584,128]{1,0:T(8,128)(2,1)S(1)}, u32[]{:S(2)}, u32[]{:S(2)}) collective-permute-start(bf16[1584,128]{1,0:T(8,128)(2,1)S(1)} %get-tuple-element.13.refs_0_), channel_id=1, source_target_pairs={{0,2},{2,4},{4,6},{1,3},{3,5},{5,7},{8,10},{10,12},{12,14},{9,11},... | collective-permute-start | bytes 1216520 | tf_op jit(solution)/shard_map/ppermute | solution.py:32
  57.7 4.6 %collective-permute-start.3 = (bf16[1584,128]{1,0:T(8,128)(2,1)S(1)}, bf16[1584,128]{1,0:T(8,128)(2,1)S(1)}, u32[]{:S(2)}, u32[]{:S(2)}) collective-permute-start(bf16[1584,128]{1,0:T(8,128)(2,1)S(1)} %get-tuple-element.13.refs_0_), channel_id=1, source_target_pairs={{2,0},{4,2},{6,4},{3,1},{5,3},{7,5},{10,8},{12,10},{14,12},{11,9},... | collective-permute-start | bytes 1216520 | tf_op jit(solution)/shard_map/ppermute | solution.py:32
  62.4 1.8 %attend.8 = bf16[1584,128]{1,0:T(8,128)(2,1)S(1)} custom-call(bf16[1584,128]{1,0:T(8,128)(2,1)S(1)} %collective-permute-done.9.refs_0_, bf16[1584,128]{1,0:T(8,128)(2,1)S(1)} %collective-permute-done.10.refs_1_, bf16[3072,128]{1,0:T(8,128)(2,1)S(1)} %collective-permute-done.6.refs_1_.refs_2_, bf16[3072,128]{1,0:T(8,128)(2,1)S(1)} %get-tuple-element.18.refs_2_.refs_3_, ...), custom_call_target="tpu_custom_call" | custom-call | flops 1000000000 | bytes 1572864 | tf_op jit(solution)/shard_map/attend/pallas_call | solution.py:280
  64.2 4.6 %collective-permute-start.11 = (bf16[1584,128]{1,0:T(8,128)(2,1)S(1)}, bf16[1584,128]{1,0:T(8,128)(2,1)S(1)}, u32[]{:S(2)}, u32[]{:S(2)}) collective-permute-start(bf16[1584,128]{1,0:T(8,128)(2,1)S(1)} %attend.8), channel_id=1, source_target_pairs={{0,8},{8,16},{16,24},{24,32},{32,40},{40,48},{48,56},{56,64},{64,7... | collective-permute-start | bytes 1216520 | tf_op jit(solution)/shard_map/ppermute | solution.py:32
  68.9 2.1 %attend.9 = bf16[1584,128]{1,0:T(8,128)(2,1)S(1)} custom-call(bf16[1584,128]{1,0:T(8,128)(2,1)S(1)} %collective-permute-done.12.refs_0_, bf16[3072,128]{1,0:T(8,128)(2,1)S(1)} %collective-permute-done.6.refs_1_.refs_2_, bf16[3072,128]{1,0:T(8,128)(2,1)S(1)} %get-tuple-element.18.refs_2_.refs_3_, ...), custom_call_target="tpu_custom_call" | custom-call | flops 1000000000 | bytes 1572864 | tf_op jit(solution)/shard_map/attend/pallas_call | solution.py:280
  70.9 2.7 %collective-permute-start.13 = (bf16[1584,128]{1,0:T(8,128)(2,1)S(1)}, bf16[1584,128]{1,0:T(8,128)(2,1)S(1)}, u32[]{:S(2)}, u32[]{:S(2)}) collective-permute-start(bf16[1584,128]{1,0:T(8,128)(2,1)S(1)} %attend.9), channel_id=1, source_target_pairs={{0,16},{8,24},{16,32},{24,40},{32,48},{40,56},{48,64},{56,72},{64,... | collective-permute-start | bytes 1216520 | tf_op jit(solution)/shard_map/ppermute | solution.py:32
  73.7 1.3 %attend.6 = (bf16[1584,128]{1,0:T(8,128)(2,1)S(1)}, bf16[1584,128]{1,0:T(8,128)(2,1)S(1)}) custom-call(bf16[1584,128]{1,0:T(8,128)(2,1)S(1)} %collective-permute-done.2.refs_0_, bf16[1584,128]{1,0:T(8,128)(2,1)S(1)} %collective-permute-done.3.refs_1_, bf16[3072,128]{1,0:T(8,128)(2,1)S(1)} %get-tuple-element.14.refs_1_.refs_2_, ...), custom_call_target="tpu_custom_call" | custom-call | flops 1000000000 | bytes 1572864 | tf_op jit(solution)/shard_map/attend/pallas_call | solution.py:280
  75.0 2.0 %collective-permute-start.4 = (bf16[1584,128]{1,0:T(8,128)(2,1)S(1)}, bf16[1584,128]{1,0:T(8,128)(2,1)S(1)}, u32[]{:S(2)}, u32[]{:S(2)}) collective-permute-start(bf16[1584,128]{1,0:T(8,128)(2,1)S(1)} %get-tuple-element.15), channel_id=1, source_target_pairs={{0,2},{2,4},{4,6},{1,3},{3,5},{5,7},{8,10},{10,12},{12,14},{9,11},... | collective-permute-start | bytes 1216520 | tf_op jit(solution)/shard_map/ppermute | solution.py:32
  76.9 4.0 %collective-permute-start.5 = (bf16[1584,128]{1,0:T(8,128)(2,1)S(1)}, bf16[1584,128]{1,0:T(8,128)(2,1)S(1)}, u32[]{:S(2)}, u32[]{:S(2)}) collective-permute-start(bf16[1584,128]{1,0:T(8,128)(2,1)S(1)} %get-tuple-element.16), channel_id=1, source_target_pairs={{2,0},{4,2},{6,4},{3,1},{5,3},{7,5},{10,8},{12,10},{14,12},{11,9},... | collective-permute-start | bytes 1216520 | tf_op jit(solution)/shard_map/ppermute | solution.py:32
  80.9 2.1 %attend.7.local = f32[776,256]{1,0:T(8,128)S(1)} custom-call(bf16[1584,128]{1,0:T(8,128)(2,1)S(1)} %get-tuple-element.17.refs_0_, bf16[3072,128]{1,0:T(8,128)(2,1)S(1)} %collective-permute-done.6.refs_1_.refs_2_, bf16[3072,128]{1,0:T(8,128)(2,1)S(1)} %get-tuple-element.18.refs_2_.refs_3_, bf16[3072,128]{1,0:T(8,128)(2,1)S(1)} %collective-permute-done.7.refs_3_.refs_4_, ...), custom_call_target="tpu_custom_call" | custom-call | flops 1000000000 | bytes 1572864 | tf_op jit(solution)/shard_map/attend/pallas_call | solution.py:280
  83.0 1.0 %finish.2.refs_2_ = bf16[1,8,32,1536]{3,2,1,0:T(8,128)(2,1)} custom-call(s32[8,128]{1,0:T(8,128)S(1)} %get-tuple-element.12.ok_ref, f32[776,256]{1,0:T(8,128)S(1)} %attend.7.local, bf16[1584,128]{1,0:T(8,128)(2,1)S(1)} %collective-permute-done.11.refs_0_, bf16[1584,128]{1,0:T(8,128)(2,1)S(1)} %collective-permute-done.13.refs_1_), custom_call_target="tpu_custom_call" | custom-call | flops 100000000 | bytes 1572864 | tf_op jit(solution)/shard_map/finish/pallas_call | solution.py:340
  84.0 0.8 attend.5.local
  84.9 1.9 %collective-permute-done.5.refs_1_ = bf16[1584,128]{1,0:T(8,128)(2,1)S(1)} collective-permute-done((bf16[1584,128]{1,0:T(8,128)(2,1)S(1)}, bf16[1584,128]{1,0:T(8,128)(2,1)S(1)}, u32[]{:S(2)}, u32[]{:S(2)}) %collective-permute-start.5) | collective-permute-done | bytes 405536 | tf_op jit(solution)/shard_map/ppermute | solution.py:32
  86.8 1.0 %finish.3 = bf16[1,8,32,1536]{3,2,1,0:T(8,128)(2,1)} custom-call(s32[8,128]{1,0:T(8,128)S(1)} %get-tuple-element.12.ok_ref, f32[776,256]{1,0:T(8,128)S(1)} %attend.5.local, bf16[1584,128]{1,0:T(8,128)(2,1)S(1)} %collective-permute-done.4.refs_0_, bf16[1584,128]{1,0:T(8,128)(2,1)S(1)} %collective-permute-done.5.refs_1_, ...), custom_call_target="tpu_custom_call", output_to_operand_aliasing={{}: (4, {})} | custom-call | flops 100000000 | bytes 1572864 | tf_op jit(solution)/shard_map/finish/pallas_call | solution.py:340
  (12 shorter events, 0.0 us)
Async XLA Ops:
  2.0 47.2 %collective-permute-start = (bf16[3072,128]{1,0:T(8,128)(2,1)S(1)}, bf16[3072,128]{1,0:T(8,128)(2,1)S(1)}, u32[]{:S(2)}, u32[]{:S(2)}) collective-permute-start(bf16[3072,128]{1,0:T(8,128)(2,1)S(1)} %get-tuple-element.14.refs_1_.refs_2_), channel_id=1, source_target_pairs={{0,8},{8,16},{16,24},{24,32},{32,40},{40,48},{48,56},{56,64},{64,7... | collective-permute-start | bytes 2359304 | tf_op jit(solution)/shard_map/ppermute | solution.py:32
  6.8 41.8 %collective-permute-start.9 = (bf16[1584,128]{1,0:T(8,128)(2,1)S(1)}, bf16[1584,128]{1,0:T(8,128)(2,1)S(1)}, u32[]{:S(2)}, u32[]{:S(2)}) collective-permute-start(bf16[1584,128]{1,0:T(8,128)(2,1)S(1)} %get-tuple-element.17.refs_0_), channel_id=1, source_target_pairs={{10,2},{12,4},{14,6},{16,8},{18,10},{20,12},{22,14},{24,16},{26,18... | collective-permute-start | bytes 1216520 | tf_op jit(solution)/shard_map/ppermute | solution.py:42
  8.1 47.6 %collective-permute-start.6 = (bf16[3072,128]{1,0:T(8,128)(2,1)S(1)}, bf16[3072,128]{1,0:T(8,128)(2,1)S(1)}, u32[]{:S(2)}, u32[]{:S(2)}) collective-permute-start(bf16[3072,128]{1,0:T(8,128)(2,1)S(1)} %get-tuple-element.18.refs_2_.refs_3_), channel_id=1, source_target_pairs={{0,2},{2,4},{4,6},{1,3},{3,5},{5,7},{8,10},{10,12},{12,14},{9,11},... | collective-permute-start | bytes 2359304 | tf_op jit(solution)/shard_map/ppermute | solution.py:32
  11.7 46.0 %collective-permute-start.7 = (bf16[3072,128]{1,0:T(8,128)(2,1)S(1)}, bf16[3072,128]{1,0:T(8,128)(2,1)S(1)}, u32[]{:S(2)}, u32[]{:S(2)}) collective-permute-start(bf16[3072,128]{1,0:T(8,128)(2,1)S(1)} %get-tuple-element.18.refs_2_.refs_3_), channel_id=1, source_target_pairs={{4,2},{6,4},{10,8},{12,10},{14,12},{18,16},{20,18},{22,20},{26,24}... | collective-permute-start | bytes 2359304 | tf_op jit(solution)/shard_map/ppermute | solution.py:42
  13.0 49.3 %collective-permute-start.8 = (bf16[3072,128]{1,0:T(8,128)(2,1)S(1)}, bf16[3072,128]{1,0:T(8,128)(2,1)S(1)}, u32[]{:S(2)}, u32[]{:S(2)}) collective-permute-start(bf16[3072,128]{1,0:T(8,128)(2,1)S(1)} %get-tuple-element.18.refs_2_.refs_3_), channel_id=1, source_target_pairs={{2,0},{3,1},{258,256},{259,257}} | collective-permute-start | bytes 2359304 | tf_op jit(solution)/shard_map/ppermute | solution.py:42
  48.6 1.4 %collective-permute-start.10 = (bf16[1584,128]{1,0:T(8,128)(2,1)S(1)}, bf16[1584,128]{1,0:T(8,128)(2,1)S(1)}, u32[]{:S(2)}, u32[]{:S(2)}) collective-permute-start(bf16[1584,128]{1,0:T(8,128)(2,1)S(1)} %get-tuple-element.17.refs_0_), channel_id=1, source_target_pairs={{8,0},{9,1},{264,256},{265,257}} | collective-permute-start | bytes 1216520 | tf_op jit(solution)/shard_map/ppermute | solution.py:42
  49.3 24.3 %collective-permute-start.1 = (bf16[3072,128]{1,0:T(8,128)(2,1)S(1)}, bf16[3072,128]{1,0:T(8,128)(2,1)S(1)}, u32[]{:S(2)}, u32[]{:S(2)}) collective-permute-start(bf16[3072,128]{1,0:T(8,128)(2,1)S(1)} %collective-permute-done.refs_2_.refs_3_), channel_id=1, source_target_pairs={{8,16},{16,24},{24,32},{32,40},{40,48},{48,56},{56,64},{64,72},{72... | collective-permute-start | bytes 2359304 | tf_op jit(solution)/shard_map/ppermute | solution.py:32
  50.0 18.8 %collective-permute-start.12 = (bf16[1584,128]{1,0:T(8,128)(2,1)S(1)}, bf16[1584,128]{1,0:T(8,128)(2,1)S(1)}, u32[]{:S(2)}, u32[]{:S(2)}) collective-permute-start(bf16[1584,128]{1,0:T(8,128)(2,1)S(1)} %collective-permute-done.9.refs_0_), channel_id=1, source_target_pairs={{8,0},{16,8},{24,16},{32,24},{40,32},{48,40},{56,48},{64,56},{72,6... | collective-permute-start | bytes 1216520 | tf_op jit(solution)/shard_map/ppermute | solution.py:32
  55.8 17.9 %collective-permute-start.2 = (bf16[1584,128]{1,0:T(8,128)(2,1)S(1)}, bf16[1584,128]{1,0:T(8,128)(2,1)S(1)}, u32[]{:S(2)}, u32[]{:S(2)}) collective-permute-start(bf16[1584,128]{1,0:T(8,128)(2,1)S(1)} %get-tuple-element.13.refs_0_), channel_id=1, source_target_pairs={{0,2},{2,4},{4,6},{1,3},{3,5},{5,7},{8,10},{10,12},{12,14},{9,11},... | collective-permute-start | bytes 1216520 | tf_op jit(solution)/shard_map/ppermute | solution.py:32
  57.7 15.9 %collective-permute-start.3 = (bf16[1584,128]{1,0:T(8,128)(2,1)S(1)}, bf16[1584,128]{1,0:T(8,128)(2,1)S(1)}, u32[]{:S(2)}, u32[]{:S(2)}) collective-permute-start(bf16[1584,128]{1,0:T(8,128)(2,1)S(1)} %get-tuple-element.13.refs_0_), channel_id=1, source_target_pairs={{2,0},{4,2},{6,4},{3,1},{5,3},{7,5},{10,8},{12,10},{14,12},{11,9},... | collective-permute-start | bytes 1216520 | tf_op jit(solution)/shard_map/ppermute | solution.py:32
  64.2 18.8 %collective-permute-start.11 = (bf16[1584,128]{1,0:T(8,128)(2,1)S(1)}, bf16[1584,128]{1,0:T(8,128)(2,1)S(1)}, u32[]{:S(2)}, u32[]{:S(2)}) collective-permute-start(bf16[1584,128]{1,0:T(8,128)(2,1)S(1)} %attend.8), channel_id=1, source_target_pairs={{0,8},{8,16},{16,24},{24,32},{32,40},{40,48},{48,56},{56,64},{64,7... | collective-permute-start | bytes 1216520 | tf_op jit(solution)/shard_map/ppermute | solution.py:32
  70.9 12.1 %collective-permute-start.13 = (bf16[1584,128]{1,0:T(8,128)(2,1)S(1)}, bf16[1584,128]{1,0:T(8,128)(2,1)S(1)}, u32[]{:S(2)}, u32[]{:S(2)}) collective-permute-start(bf16[1584,128]{1,0:T(8,128)(2,1)S(1)} %attend.9), channel_id=1, source_target_pairs={{0,16},{8,24},{16,32},{24,40},{32,48},{40,56},{48,64},{56,72},{64,... | collective-permute-start | bytes 1216520 | tf_op jit(solution)/shard_map/ppermute | solution.py:32
  75.0 9.9 %collective-permute-start.4 = (bf16[1584,128]{1,0:T(8,128)(2,1)S(1)}, bf16[1584,128]{1,0:T(8,128)(2,1)S(1)}, u32[]{:S(2)}, u32[]{:S(2)}) collective-permute-start(bf16[1584,128]{1,0:T(8,128)(2,1)S(1)} %get-tuple-element.15), channel_id=1, source_target_pairs={{0,2},{2,4},{4,6},{1,3},{3,5},{5,7},{8,10},{10,12},{12,14},{9,11},... | collective-permute-start | bytes 1216520 | tf_op jit(solution)/shard_map/ppermute | solution.py:32
  76.9 9.8 %collective-permute-start.5 = (bf16[1584,128]{1,0:T(8,128)(2,1)S(1)}, bf16[1584,128]{1,0:T(8,128)(2,1)S(1)}, u32[]{:S(2)}, u32[]{:S(2)}) collective-permute-start(bf16[1584,128]{1,0:T(8,128)(2,1)S(1)} %get-tuple-element.16), channel_id=1, source_target_pairs={{2,0},{4,2},{6,4},{3,1},{5,3},{7,5},{10,8},{12,10},{14,12},{11,9},... | collective-permute-start | bytes 1216520 | tf_op jit(solution)/shard_map/ppermute | solution.py:32

commit v5 on v4

--- a/solution.py
+++ b/solution.py
@@ -386,19 +386,18 @@
     (ka,) = go((frames[1],), mine, frame_cases, qs=(qa,), kvs=along)
 
     grid = ("tm", "space")
-    below, beside = (1, 0), (0, 1)
+    below = (1, 0)
     q1 = hop(qb, grid, (-1, 0), lambda place: place != below)
     q1_late = hop(qb, grid, (-1, 0), lambda place: place == below)
-    hi = hop(kvb, grid, (0, -1), lambda place: place != beside)
-    hi_late = hop(kvb, grid, (0, -1), lambda place: place == beside)
+    hi = shift(kvb, "space", -1)
     q2 = shift(q1, "tm", -1, ahead=1)
     lo = shift(kvb, "space", 1)
-    across = (lo, kvb, hi, hi_late)
-    offsets = [tuple(3 * back + dy for dy in (0, 1, 2, 2)) for back in range(3)]
+    across = (lo, kvb, hi)
+    offsets = [tuple(3 * back + dy for dy in range(3)) for back in range(3)]
 
     def row_cases(late=0):
         return (
-            ((first, edge), (late,), (1, 3)),
+            ((first, edge), (late,), (1, 2)),
             ((edge,), (0,), (1, 2)),
             ((("space", -1),), (0,), (0, 1)),
             ((), (0,), (0, 1, 2)),

time: 88.4 us -> 89.3 us (1.010)
  the two profiles are of different devices: /device:TPU:34 before, /device:TPU:288 now
where the time goes in v5:
time: 89.3 us; the launch traced here: 88.8 us
  starting transfers between devices  56.5 us (63%)
  waiting for transfers between devices  18.2 us (20%)
  Pallas kernels  13.7 us (15%)
    ppermute x11, starting transfers between devices, shift(): return lax.ppermute(block, axis, route)  53.8 us
    ppermute x11, waiting for transfers between devices, shift(): return lax.ppermute(block, axis, route)  18.2 us
    pallas_call x5, Pallas kernels, attend(): pl.pallas_call(functools.partial(attend_kernel, heads, tokens, cols, sets...  9.71 us
    ppermute x2, starting transfers between devices, hop(): return lax.ppermute(block, axes, route)  2.64 us
    pallas_call x1, Pallas kernels, pack(): pl.pallas_call(functools.partial(pack_kernel, heads, tokens), out_shape=s...  2.04 us
    pallas_call x2, Pallas kernels, finish(): pl.pallas_call(functools.partial(finish_kernel, heads, tokens, cols, firs...  1.97 us
  transfers between devices with their start and end apart: 13, of which 3 were waited for; matrix products, arithmetic and copies ran while one was open for 0% of the time, Pallas kernels for 12%

profile of v5, /device:TPU:288, one launch (start us, length us, event | category | flops | bytes accessed | tf_op | source)
XLA Modules:
  0.0 88.8 jit_solution(8074723243126593420)
XLA Ops:
  0.0 2.0 %pack.1 = (bf16[1584,128]{1,0:T(8,128)(2,1)S(1)}, bf16[3072,128]{1,0:T(8,128)(2,1)S(1)}, bf16[1584,128]{1,0:T(8,128)(2,1)S(1)}, bf16[3072,128]{1,0:T(8,128)(2,1)S(1)}, s32[8,128]{1,0:T(8,128)S(1)}) custom-call(bf16[1,8,32,1536]{3,2,1,0:T(8,128)(2,1)} %q_ref.1, bf16[1,8,32,1536]{3,2,1,0:T(8,128)(2,1)} %k_ref.1, bf16[1,8,32,1536]{3,2,1,0:T(8,128)(2,1)} %v_ref.1, ...), custom_call_target="tpu_custom_call" | custom-call | flops 1000000000 | bytes 2359296 | tf_op jit(solution)/shard_map/pack/pallas_call | solution.py:118
  2.0 4.7 %collective-permute-start = (bf16[3072,128]{1,0:T(8,128)(2,1)S(1)}, bf16[3072,128]{1,0:T(8,128)(2,1)S(1)}, u32[]{:S(2)}, u32[]{:S(2)}) collective-permute-start(bf16[3072,128]{1,0:T(8,128)(2,1)S(1)} %get-tuple-element.14.refs_1_.refs_2_), channel_id=1, source_target_pairs={{0,8},{8,16},{16,24},{24,32},{32,40},{40,48},{48,56},{56,64},{64,7... | collective-permute-start | bytes 2359304 | tf_op jit(solution)/shard_map/ppermute | solution.py:32
  6.8 3.6 %collective-permute-start.6 = (bf16[3072,128]{1,0:T(8,128)(2,1)S(1)}, bf16[3072,128]{1,0:T(8,128)(2,1)S(1)}, u32[]{:S(2)}, u32[]{:S(2)}) collective-permute-start(bf16[3072,128]{1,0:T(8,128)(2,1)S(1)} %get-tuple-element.18.refs_2_.refs_3_), channel_id=1, source_target_pairs={{0,2},{2,4},{4,6},{1,3},{3,5},{5,7},{8,10},{10,12},{12,14},{9,11},... | collective-permute-start | bytes 2359304 | tf_op jit(solution)/shard_map/ppermute | solution.py:32
  10.4 1.3 %collective-permute-start.7 = (bf16[3072,128]{1,0:T(8,128)(2,1)S(1)}, bf16[3072,128]{1,0:T(8,128)(2,1)S(1)}, u32[]{:S(2)}, u32[]{:S(2)}) collective-permute-start(bf16[3072,128]{1,0:T(8,128)(2,1)S(1)} %get-tuple-element.18.refs_2_.refs_3_), channel_id=1, source_target_pairs={{2,0},{4,2},{6,4},{3,1},{5,3},{7,5},{10,8},{12,10},{14,12},{11,9},... | collective-permute-start | bytes 2359304 | tf_op jit(solution)/shard_map/ppermute | solution.py:32
  11.7 2.0 %collective-permute-start.8 = (bf16[1584,128]{1,0:T(8,128)(2,1)S(1)}, bf16[1584,128]{1,0:T(8,128)(2,1)S(1)}, u32[]{:S(2)}, u32[]{:S(2)}) collective-permute-start(bf16[1584,128]{1,0:T(8,128)(2,1)S(1)} %get-tuple-element.17.refs_0_), channel_id=1, source_target_pairs={{10,2},{12,4},{14,6},{16,8},{18,10},{20,12},{22,14},{24,16},{26,18... | collective-permute-start | bytes 1216520 | tf_op jit(solution)/shard_map/ppermute | solution.py:42
  13.7 0.7 collective-permute-start.9
  14.4 10.0 %collective-permute-done.refs_2_.refs_3_ = bf16[3072,128]{1,0:T(8,128)(2,1)S(1)} collective-permute-done((bf16[3072,128]{1,0:T(8,128)(2,1)S(1)}, bf16[3072,128]{1,0:T(8,128)(2,1)S(1)}, u32[]{:S(2)}, u32[]{:S(2)}) %collective-permute-start) | collective-permute-done | bytes 786464 | tf_op jit(solution)/shard_map/ppermute | solution.py:32
  24.3 5.7 %collective-permute-start.1 = (bf16[3072,128]{1,0:T(8,128)(2,1)S(1)}, bf16[3072,128]{1,0:T(8,128)(2,1)S(1)}, u32[]{:S(2)}, u32[]{:S(2)}) collective-permute-start(bf16[3072,128]{1,0:T(8,128)(2,1)S(1)} %collective-permute-done.refs_2_.refs_3_), channel_id=1, source_target_pairs={{8,16},{16,24},{24,32},{32,40},{40,48},{48,56},{56,64},{64,72},{72... | collective-permute-start | bytes 2359304 | tf_op jit(solution)/shard_map/ppermute | solution.py:32
  30.1 27.0 %collective-permute-start.11 = (bf16[1584,128]{1,0:T(8,128)(2,1)S(1)}, bf16[1584,128]{1,0:T(8,128)(2,1)S(1)}, u32[]{:S(2)}, u32[]{:S(2)}) collective-permute-start(bf16[1584,128]{1,0:T(8,128)(2,1)S(1)} %collective-permute-done.8.refs_0_), channel_id=1, source_target_pairs={{8,0},{16,8},{24,16},{32,24},{40,32},{48,40},{56,48},{64,56},{72,6... | collective-permute-start | bytes 1216520 | tf_op jit(solution)/shard_map/ppermute | solution.py:32
  57.1 1.4 %collective-permute-start.2 = (bf16[1584,128]{1,0:T(8,128)(2,1)S(1)}, bf16[1584,128]{1,0:T(8,128)(2,1)S(1)}, u32[]{:S(2)}, u32[]{:S(2)}) collective-permute-start(bf16[1584,128]{1,0:T(8,128)(2,1)S(1)} %get-tuple-element.13.refs_0_), channel_id=1, source_target_pairs={{0,2},{2,4},{4,6},{1,3},{3,5},{5,7},{8,10},{10,12},{12,14},{9,11},... | collective-permute-start | bytes 1216520 | tf_op jit(solution)/shard_map/ppermute | solution.py:32
  58.5 1.3 %collective-permute-start.3 = (bf16[1584,128]{1,0:T(8,128)(2,1)S(1)}, bf16[1584,128]{1,0:T(8,128)(2,1)S(1)}, u32[]{:S(2)}, u32[]{:S(2)}) collective-permute-start(bf16[1584,128]{1,0:T(8,128)(2,1)S(1)} %get-tuple-element.13.refs_0_), channel_id=1, source_target_pairs={{2,0},{4,2},{6,4},{3,1},{5,3},{7,5},{10,8},{12,10},{14,12},{11,9},... | collective-permute-start | bytes 1216520 | tf_op jit(solution)/shard_map/ppermute | solution.py:32
  59.9 1.3 %attend.8 = bf16[1584,128]{1,0:T(8,128)(2,1)S(1)} custom-call(bf16[1584,128]{1,0:T(8,128)(2,1)S(1)} %collective-permute-done.8.refs_0_, bf16[1584,128]{1,0:T(8,128)(2,1)S(1)} %collective-permute-done.9.refs_1_, bf16[3072,128]{1,0:T(8,128)(2,1)S(1)} %collective-permute-done.6.refs_1_.refs_2_, bf16[3072,128]{1,0:T(8,128)(2,1)S(1)} %get-tuple-element.18.refs_2_.refs_3_, ...), custom_call_target="tpu_custom_call" | custom-call | flops 1000000000 | bytes 1572864 | tf_op jit(solution)/shard_map/attend/pallas_call | solution.py:280
  61.2 2.0 %collective-permute-start.10 = (bf16[1584,128]{1,0:T(8,128)(2,1)S(1)}, bf16[1584,128]{1,0:T(8,128)(2,1)S(1)}, u32[]{:S(2)}, u32[]{:S(2)}) collective-permute-start(bf16[1584,128]{1,0:T(8,128)(2,1)S(1)} %attend.8), channel_id=1, source_target_pairs={{0,8},{8,16},{16,24},{24,32},{32,40},{40,48},{48,56},{56,64},{64,7... | collective-permute-start | bytes 1216520 | tf_op jit(solution)/shard_map/ppermute | solution.py:32
  63.2 1.5 %attend.9 = bf16[1584,128]{1,0:T(8,128)(2,1)S(1)} custom-call(bf16[1584,128]{1,0:T(8,128)(2,1)S(1)} %collective-permute-done.11.refs_0_, bf16[3072,128]{1,0:T(8,128)(2,1)S(1)} %collective-permute-done.6.refs_1_.refs_2_, bf16[3072,128]{1,0:T(8,128)(2,1)S(1)} %get-tuple-element.18.refs_2_.refs_3_, bf16[3072,128]{1,0:T(8,128)(2,1)S(1)} %collective-permute-done.7.refs_3_.refs_4_), custom_call_target="tpu_custom_call" | custom-call | flops 1000000000 | bytes 1572864 | tf_op jit(solution)/shard_map/attend/pallas_call | solution.py:280
  64.7 2.0 %collective-permute-start.12 = (bf16[1584,128]{1,0:T(8,128)(2,1)S(1)}, bf16[1584,128]{1,0:T(8,128)(2,1)S(1)}, u32[]{:S(2)}, u32[]{:S(2)}) collective-permute-start(bf16[1584,128]{1,0:T(8,128)(2,1)S(1)} %attend.9), channel_id=1, source_target_pairs={{0,16},{8,24},{16,32},{24,40},{32,48},{40,56},{48,64},{56,72},{64,... | collective-permute-start | bytes 1216520 | tf_op jit(solution)/shard_map/ppermute | solution.py:32
  66.7 4.1 %collective-permute-done.3.refs_1_ = bf16[1584,128]{1,0:T(8,128)(2,1)S(1)} collective-permute-done((bf16[1584,128]{1,0:T(8,128)(2,1)S(1)}, bf16[1584,128]{1,0:T(8,128)(2,1)S(1)}, u32[]{:S(2)}, u32[]{:S(2)}) %collective-permute-start.3) | collective-permute-done | bytes 405536 | tf_op jit(solution)/shard_map/ppermute | solution.py:32
  70.8 3.4 %attend.6 = (bf16[1584,128]{1,0:T(8,128)(2,1)S(1)}, bf16[1584,128]{1,0:T(8,128)(2,1)S(1)}) custom-call(bf16[1584,128]{1,0:T(8,128)(2,1)S(1)} %collective-permute-done.2.refs_0_, bf16[1584,128]{1,0:T(8,128)(2,1)S(1)} %collective-permute-done.3.refs_1_, bf16[3072,128]{1,0:T(8,128)(2,1)S(1)} %get-tuple-element.14.refs_1_.refs_2_, ...), custom_call_target="tpu_custom_call" | custom-call | flops 1000000000 | bytes 1572864 | tf_op jit(solution)/shard_map/attend/pallas_call | solution.py:280
  74.2 3.6 %collective-permute-start.4 = (bf16[1584,128]{1,0:T(8,128)(2,1)S(1)}, bf16[1584,128]{1,0:T(8,128)(2,1)S(1)}, u32[]{:S(2)}, u32[]{:S(2)}) collective-permute-start(bf16[1584,128]{1,0:T(8,128)(2,1)S(1)} %get-tuple-element.15), channel_id=1, source_target_pairs={{0,2},{2,4},{4,6},{1,3},{3,5},{5,7},{8,10},{10,12},{12,14},{9,11},... | collective-permute-start | bytes 1216520 | tf_op jit(solution)/shard_map/ppermute | solution.py:32
  77.8 1.3 %collective-permute-start.5 = (bf16[1584,128]{1,0:T(8,128)(2,1)S(1)}, bf16[1584,128]{1,0:T(8,128)(2,1)S(1)}, u32[]{:S(2)}, u32[]{:S(2)}) collective-permute-start(bf16[1584,128]{1,0:T(8,128)(2,1)S(1)} %get-tuple-element.16), channel_id=1, source_target_pairs={{2,0},{4,2},{6,4},{3,1},{5,3},{7,5},{10,8},{12,10},{14,12},{11,9},... | collective-permute-start | bytes 1216520 | tf_op jit(solution)/shard_map/ppermute | solution.py:32
  79.1 1.6 %attend.7.local = f32[776,256]{1,0:T(8,128)S(1)} custom-call(bf16[1584,128]{1,0:T(8,128)(2,1)S(1)} %get-tuple-element.17.refs_0_, bf16[3072,128]{1,0:T(8,128)(2,1)S(1)} %collective-permute-done.6.refs_1_.refs_2_, bf16[3072,128]{1,0:T(8,128)(2,1)S(1)} %get-tuple-element.18.refs_2_.refs_3_, bf16[3072,128]{1,0:T(8,128)(2,1)S(1)} %collective-permute-done.7.refs_3_.refs_4_), custom_call_target="tpu_custom_call" | custom-call | flops 1000000000 | bytes 1572864 | tf_op jit(solution)/shard_map/attend/pallas_call | solution.py:280
  80.7 1.0 %finish.2.refs_2_ = bf16[1,8,32,1536]{3,2,1,0:T(8,128)(2,1)} custom-call(s32[8,128]{1,0:T(8,128)S(1)} %get-tuple-element.12.ok_ref, f32[776,256]{1,0:T(8,128)S(1)} %attend.7.local, bf16[1584,128]{1,0:T(8,128)(2,1)S(1)} %collective-permute-done.10.refs_0_, bf16[1584,128]{1,0:T(8,128)(2,1)S(1)} %collective-permute-done.12.refs_1_), custom_call_target="tpu_custom_call" | custom-call | flops 100000000 | bytes 1572864 | tf_op jit(solution)/shard_map/finish/pallas_call | solution.py:340
  81.7 1.9 %attend.5.local = f32[776,256]{1,0:T(8,128)S(1)} custom-call(bf16[1584,128]{1,0:T(8,128)(2,1)S(1)} %get-tuple-element.13.refs_0_, bf16[3072,128]{1,0:T(8,128)(2,1)S(1)} %get-tuple-element.14.refs_1_.refs_2_, bf16[3072,128]{1,0:T(8,128)(2,1)S(1)} %collective-permute-done.refs_2_.refs_3_, bf16[3072,128]{1,0:T(8,128)(2,1)S(1)} %collective-permute-done.1.refs_3_.refs_4_), custom_call_target="tpu_custom_call" | custom-call | flops 1000000000 | bytes 1572864 | tf_op jit(solution)/shard_map/attend/pallas_call | solution.py:280
  83.5 4.1 %collective-permute-done.5.refs_1_ = bf16[1584,128]{1,0:T(8,128)(2,1)S(1)} collective-permute-done((bf16[1584,128]{1,0:T(8,128)(2,1)S(1)}, bf16[1584,128]{1,0:T(8,128)(2,1)S(1)}, u32[]{:S(2)}, u32[]{:S(2)}) %collective-permute-start.5) | collective-permute-done | bytes 405536 | tf_op jit(solution)/shard_map/ppermute | solution.py:32
  87.6 1.0 %finish.3 = bf16[1,8,32,1536]{3,2,1,0:T(8,128)(2,1)} custom-call(s32[8,128]{1,0:T(8,128)S(1)} %get-tuple-element.12.ok_ref, f32[776,256]{1,0:T(8,128)S(1)} %attend.5.local, bf16[1584,128]{1,0:T(8,128)(2,1)S(1)} %collective-permute-done.4.refs_0_, bf16[1584,128]{1,0:T(8,128)(2,1)S(1)} %collective-permute-done.5.refs_1_, ...), custom_call_target="tpu_custom_call", output_to_operand_aliasing={{}: (4, {})} | custom-call | flops 100000000 | bytes 1572864 | tf_op jit(solution)/shard_map/finish/pallas_call | solution.py:340
  (10 shorter events, 0.0 us)
Async XLA Ops:
  2.0 22.3 %collective-permute-start = (bf16[3072,128]{1,0:T(8,128)(2,1)S(1)}, bf16[3072,128]{1,0:T(8,128)(2,1)S(1)}, u32[]{:S(2)}, u32[]{:S(2)}) collective-permute-start(bf16[3072,128]{1,0:T(8,128)(2,1)S(1)} %get-tuple-element.14.refs_1_.refs_2_), channel_id=1, source_target_pairs={{0,8},{8,16},{16,24},{24,32},{32,40},{40,48},{48,56},{56,64},{64,7... | collective-permute-start | bytes 2359304 | tf_op jit(solution)/shard_map/ppermute | solution.py:32
  6.8 51.7 %collective-permute-start.6 = (bf16[3072,128]{1,0:T(8,128)(2,1)S(1)}, bf16[3072,128]{1,0:T(8,128)(2,1)S(1)}, u32[]{:S(2)}, u32[]{:S(2)}) collective-permute-start(bf16[3072,128]{1,0:T(8,128)(2,1)S(1)} %get-tuple-element.18.refs_2_.refs_3_), channel_id=1, source_target_pairs={{0,2},{2,4},{4,6},{1,3},{3,5},{5,7},{8,10},{10,12},{12,14},{9,11},... | collective-permute-start | bytes 2359304 | tf_op jit(solution)/shard_map/ppermute | solution.py:32
  10.4 49.5 %collective-permute-start.7 = (bf16[3072,128]{1,0:T(8,128)(2,1)S(1)}, bf16[3072,128]{1,0:T(8,128)(2,1)S(1)}, u32[]{:S(2)}, u32[]{:S(2)}) collective-permute-start(bf16[3072,128]{1,0:T(8,128)(2,1)S(1)} %get-tuple-element.18.refs_2_.refs_3_), channel_id=1, source_target_pairs={{2,0},{4,2},{6,4},{3,1},{5,3},{7,5},{10,8},{12,10},{14,12},{11,9},... | collective-permute-start | bytes 2359304 | tf_op jit(solution)/shard_map/ppermute | solution.py:32
  11.7 18.4 %collective-permute-start.8 = (bf16[1584,128]{1,0:T(8,128)(2,1)S(1)}, bf16[1584,128]{1,0:T(8,128)(2,1)S(1)}, u32[]{:S(2)}, u32[]{:S(2)}) collective-permute-start(bf16[1584,128]{1,0:T(8,128)(2,1)S(1)} %get-tuple-element.17.refs_0_), channel_id=1, source_target_pairs={{10,2},{12,4},{14,6},{16,8},{18,10},{20,12},{22,14},{24,16},{26,18... | collective-permute-start | bytes 1216520 | tf_op jit(solution)/shard_map/ppermute | solution.py:42
  13.7 43.4 %collective-permute-start.9 = (bf16[1584,128]{1,0:T(8,128)(2,1)S(1)}, bf16[1584,128]{1,0:T(8,128)(2,1)S(1)}, u32[]{:S(2)}, u32[]{:S(2)}) collective-permute-start(bf16[1584,128]{1,0:T(8,128)(2,1)S(1)} %get-tuple-element.17.refs_0_), channel_id=1, source_target_pairs={{8,0},{9,1},{264,256},{265,257}} | collective-permute-start | bytes 1216520 | tf_op jit(solution)/shard_map/ppermute | solution.py:42
  24.3 46.4 %collective-permute-start.1 = (bf16[3072,128]{1,0:T(8,128)(2,1)S(1)}, bf16[3072,128]{1,0:T(8,128)(2,1)S(1)}, u32[]{:S(2)}, u32[]{:S(2)}) collective-permute-start(bf16[3072,128]{1,0:T(8,128)(2,1)S(1)} %collective-permute-done.refs_2_.refs_3_), channel_id=1, source_target_pairs={{8,16},{16,24},{24,32},{32,40},{40,48},{48,56},{56,64},{64,72},{72... | collective-permute-start | bytes 2359304 | tf_op jit(solution)/shard_map/ppermute | solution.py:32
  30.1 33.0 %collective-permute-start.11 = (bf16[1584,128]{1,0:T(8,128)(2,1)S(1)}, bf16[1584,128]{1,0:T(8,128)(2,1)S(1)}, u32[]{:S(2)}, u32[]{:S(2)}) collective-permute-start(bf16[1584,128]{1,0:T(8,128)(2,1)S(1)} %collective-permute-done.8.refs_0_), channel_id=1, source_target_pairs={{8,0},{16,8},{24,16},{32,24},{40,32},{48,40},{56,48},{64,56},{72,6... | collective-permute-start | bytes 1216520 | tf_op jit(solution)/shard_map/ppermute | solution.py:32
  57.1 9.6 %collective-permute-start.2 = (bf16[1584,128]{1,0:T(8,128)(2,1)S(1)}, bf16[1584,128]{1,0:T(8,128)(2,1)S(1)}, u32[]{:S(2)}, u32[]{:S(2)}) collective-permute-start(bf16[1584,128]{1,0:T(8,128)(2,1)S(1)} %get-tuple-element.13.refs_0_), channel_id=1, source_target_pairs={{0,2},{2,4},{4,6},{1,3},{3,5},{5,7},{8,10},{10,12},{12,14},{9,11},... | collective-permute-start | bytes 1216520 | tf_op jit(solution)/shard_map/ppermute | solution.py:32
  58.5 12.2 %collective-permute-start.3 = (bf16[1584,128]{1,0:T(8,128)(2,1)S(1)}, bf16[1584,128]{1,0:T(8,128)(2,1)S(1)}, u32[]{:S(2)}, u32[]{:S(2)}) collective-permute-start(bf16[1584,128]{1,0:T(8,128)(2,1)S(1)} %get-tuple-element.13.refs_0_), channel_id=1, source_target_pairs={{2,0},{4,2},{6,4},{3,1},{5,3},{7,5},{10,8},{12,10},{14,12},{11,9},... | collective-permute-start | bytes 1216520 | tf_op jit(solution)/shard_map/ppermute | solution.py:32
  61.2 19.5 %collective-permute-start.10 = (bf16[1584,128]{1,0:T(8,128)(2,1)S(1)}, bf16[1584,128]{1,0:T(8,128)(2,1)S(1)}, u32[]{:S(2)}, u32[]{:S(2)}) collective-permute-start(bf16[1584,128]{1,0:T(8,128)(2,1)S(1)} %attend.8), channel_id=1, source_target_pairs={{0,8},{8,16},{16,24},{24,32},{32,40},{40,48},{48,56},{56,64},{64,7... | collective-permute-start | bytes 1216520 | tf_op jit(solution)/shard_map/ppermute | solution.py:32
  64.7 16.0 %collective-permute-start.12 = (bf16[1584,128]{1,0:T(8,128)(2,1)S(1)}, bf16[1584,128]{1,0:T(8,128)(2,1)S(1)}, u32[]{:S(2)}, u32[]{:S(2)}) collective-permute-start(bf16[1584,128]{1,0:T(8,128)(2,1)S(1)} %attend.9), channel_id=1, source_target_pairs={{0,16},{8,24},{16,32},{24,40},{32,48},{40,56},{48,64},{56,72},{64,... | collective-permute-start | bytes 1216520 | tf_op jit(solution)/shard_map/ppermute | solution.py:32
  74.2 9.3 %collective-permute-start.4 = (bf16[1584,128]{1,0:T(8,128)(2,1)S(1)}, bf16[1584,128]{1,0:T(8,128)(2,1)S(1)}, u32[]{:S(2)}, u32[]{:S(2)}) collective-permute-start(bf16[1584,128]{1,0:T(8,128)(2,1)S(1)} %get-tuple-element.15), channel_id=1, source_target_pairs={{0,2},{2,4},{4,6},{1,3},{3,5},{5,7},{8,10},{10,12},{12,14},{9,11},... | collective-permute-start | bytes 1216520 | tf_op jit(solution)/shard_map/ppermute | solution.py:32
  77.8 9.8 %collective-permute-start.5 = (bf16[1584,128]{1,0:T(8,128)(2,1)S(1)}, bf16[1584,128]{1,0:T(8,128)(2,1)S(1)}, u32[]{:S(2)}, u32[]{:S(2)}) collective-permute-start(bf16[1584,128]{1,0:T(8,128)(2,1)S(1)} %get-tuple-element.16), channel_id=1, source_target_pairs={{2,0},{4,2},{6,4},{3,1},{5,3},{7,5},{10,8},{12,10},{14,12},{11,9},... | collective-permute-start | bytes 1216520 | tf_op jit(solution)/shard_map/ppermute | solution.py:32
